TPU v7x, 256 devices: a whole 4x4x8 slice. The times are simulated.
256 devices in a mesh: batch: 2 (over x_hi), items: 128 (over z, x_lo, y, core).
Axes of the slice: x: 4 (x_hi: 2, x_lo: 2; x = x_hi * 2 + x_lo), y: 4, z: 8, core: 2. Of those that a mesh axis runs over, the one named last changes fastest.
Arguments:
- users: bfloat16 [10240, 256], P(('batch', 'items')), may hold values from -6 to 6
- items: bfloat16 [65536, 256], P(('batch', 'items')), may hold values from -6 to 6
- pos_ids: int32 [10240], P(('batch', 'items')), may hold values from 0 to 65535
Outputs:
- loss: float32 [10240], P(('batch', 'items'))
- user_grad: float32 [10240, 256], P(('batch', 'items'))
- item_grad: float32 [65536, 256], P(('batch', 'items'))
All inputs are finite; a program needn't handle non-finite values.
Results may differ from a plain program's by a relative error of at most 0.0015.
Values may be sent and summed in bfloat16 or wider, within the bound.
A program may use at most 64 MiB of HBM per device.

v0:
```python
import math

import jax
import jax.numpy as jnp
from jax import lax
from jax.sharding import Mesh
from jax.sharding import PartitionSpec as P

ITEMS = ("items_0", "items_1", "items_2", "items_3")
BATCH_ITEMS = ("batch", "items_0", "items_1", "items_2", "items_3")


def joined_along(blocks, dim):
    blocks = jnp.moveaxis(blocks, 0, dim)
    lengths = blocks.shape
    return blocks.reshape(*lengths[:dim], lengths[dim] * lengths[dim + 1], *lengths[dim + 2 :])


def copy_for_each(value, axis):
    size = lax.axis_size(axis)
    return lax.all_to_all(
        jnp.broadcast_to(value[None], (size, *value.shape)), axis, 0, 0, tiled=True
    )


def collect(value, axis, dim):
    return joined_along(copy_for_each(value, axis), dim)


def all_in_one(value, axis):
    leaves = jax.tree.leaves(value)
    order = sorted(range(len(leaves)), key=lambda k: -leaves[k].size)
    width = (1, *leaves[order[0]].shape)[-1]
    lines = [
        jnp.pad(leaves[k].reshape(-1), (0, -leaves[k].size % width)).reshape(-1, width)
        for k in order
    ]
    both, at, found = (lax.all_gather(jnp.concatenate(lines), axis), 0, {})
    for k, line in zip(order, lines):
        slab = both[:, at : at + len(line)].reshape(len(both), -1)
        found[k] = slab[:, : leaves[k].size].reshape(-1, *leaves[k].shape)
        at += len(line)
    numbers = iter(range(len(leaves)))
    return jax.tree.map(lambda _: found[next(numbers)], value)


def combined_by_axis(value, axes, combine):
    for axis in axes:
        pieces = all_in_one(value, axis)
        value = jax.tree.map(lambda part: part[0], pieces)
        for k in range(1, lax.axis_size(axis)):
            value = combine(value, jax.tree.map(lambda part: part[k], pieces))
    return value


def cut_along(value, dim, size):
    lengths = value.shape
    blocks = value.reshape(*lengths[:dim], size, lengths[dim] // size, *lengths[dim + 1 :])
    return jnp.moveaxis(blocks, dim, 0)


def summed_rows(value, chips, core, dim):
    sizes = (lax.axis_size(chips), lax.axis_size(core))
    blocks = cut_along(value, dim, sizes[0] * sizes[1])
    inside = blocks.shape[1:]
    blocks = blocks.reshape(*sizes, *inside).swapaxes(0, 1).reshape(-1, *inside)
    blocks = lax.psum_scatter(blocks, core, scatter_dimension=0, tiled=True)
    return lax.psum_scatter(blocks, chips, scatter_dimension=0, tiled=True)[0]


def summed_on_arrival(value, axis, dim):
    blocks = cut_along(value, dim, lax.axis_size(axis))
    arrived = lax.all_to_all(blocks, axis, split_axis=0, concat_axis=0, tiled=True)
    return arrived.sum(axis=0)


def combine(first, second):
    top = jnp.maximum(first[0], second[0])
    total = first[1] * jnp.exp(first[0] - top) + second[1] * jnp.exp(second[0] - top)
    return (top, total, first[2] + second[2])


def block_logits(ublk, bank):
    return lax.dot_general(ublk, bank, (((1,), (1,)), ((), ())), preferred_element_type=jnp.float32)


def local(users, items, pos_ids):
    width = users.shape[1]
    own = users.shape[0]
    per_bank = items.shape[0]
    groups = lax.axis_size(ITEMS)
    group_index = lax.axis_index(ITEMS)
    bank = collect(items, "batch", 0)
    seen, seen_ids = (
        lax.all_gather(users, ITEMS, axis=0, tiled=True),
        lax.all_gather(pos_ids, ITEMS, axis=0, tiled=True),
    )
    row_base = group_index * own
    owner = seen_ids // per_bank
    offset = seen_ids % per_bank
    column = jnp.where(
        owner == group_index,
        offset,
        jnp.where(owner == group_index + groups, offset + per_bank, -1),
    )
    rows = seen.shape[0]
    size = math.gcd(rows, 1024)
    count = rows // size
    user_blocks = seen.reshape(count, size, width)
    col_blocks = column.astype(jnp.int32).reshape(count, size)
    cols = jnp.arange(bank.shape[0], dtype=jnp.int32)

    def local_stats(args):
        ublk, cblk = args
        logit = block_logits(ublk, bank)
        mask = cblk[:, None] == cols[None, :]
        peak = jnp.max(logit, axis=1)
        total = jnp.sum(jnp.exp(logit - peak[:, None]), axis=1)
        positive = jnp.sum(jnp.where(mask, logit, 0.0), axis=1)
        return (peak, total, positive)

    peak, total, positive = lax.map(local_stats, (user_blocks, col_blocks))
    peak = peak.reshape(rows)
    total = total.reshape(rows)
    positive = positive.reshape(rows)
    peak, total, positive = combined_by_axis((peak, total, positive), ITEMS, combine)
    lse = peak + jnp.log(total)

    def backward(carry, args):
        ublk, cblk, lblk = args
        logit = block_logits(ublk, bank)
        mask = cblk[:, None] == cols[None, :]
        weights = (jnp.exp(logit - lblk[:, None]) - jnp.where(mask, 1.0, 0.0)).astype(jnp.bfloat16)
        ugrad = jnp.dot(weights, bank, preferred_element_type=jnp.float32)
        carry = carry + lax.dot_general(
            weights, ublk, (((0,), (0,)), ((), ())), preferred_element_type=jnp.float32
        )
        return (carry, ugrad)

    start = jnp.zeros((bank.shape[0], width), jnp.float32)
    bank_grad, terms = lax.scan(
        backward, start, (user_blocks, col_blocks, lse.reshape(count, size))
    )
    terms = terms.reshape(rows, width)
    user_grad = summed_rows(terms, ("items_0", "items_1", "items_2"), "items_3", 0)
    item_grad = summed_on_arrival(bank_grad, "batch", 0)
    loss = lax.dynamic_slice_in_dim(lse - positive, row_base, own, 0)
    return (loss, user_grad, item_grad)


def solution(mesh):
    torus = Mesh(
        mesh.devices.reshape(mesh.shape["batch"], 8, 2, 4, 2),
        ("batch", "items_0", "items_1", "items_2", "items_3"),
    )
    return jax.shard_map(
        local,
        mesh=torus,
        in_specs=(P(BATCH_ITEMS, None), P(BATCH_ITEMS, None), P(BATCH_ITEMS)),
        out_specs=(P(BATCH_ITEMS), P(BATCH_ITEMS, None), P(BATCH_ITEMS, None)),
        check_vma=False,
    )
```

profile of v0, /device:TPU:2, one launch (start us, length us, event | category | flops | bytes accessed | tf_op | source)
XLA Modules:
  0.0 1005.7 jit_solution(12930875114837464501)
XLA Ops:
  7.9 1.6 broadcast_in_dim.46
  9.5 3.4 all-to-all-start
  15.9 535.8 %all-reduce = s32[5120]{0:T(1024)S(1)} all-reduce(s32[5120]{0:T(1024)S(1)} %dynamic-update-slice), channel_id=1, replica_groups=mesh['batch'=2,'items_0'=8,'items_1'=2,'items_2'=4,'items_3'=2] {'items_..., use_global_device_ids=true, to_apply=%add | all-reduce | flops 5120 | bytes 40960
  551.8 12.3 %while.28 = (s32[]{:T(128)}, f32[5,1024]{1,0:T(8,128)S(1)}, f32[5,1024]{1,0:T(8,128)S(1)}, f32[5,1024]{1,0:T(8,128)S(1)}, bf16[5,1024,256]{2,1,0:T(8,128)(2,1)},...) while((s32[]{:T(128)}, f32[5,1024]{1,0:T(8,128)S(1)}, ...), condition=%wide.region_4.5_spmd.clone, body=%wide.region_0.4_spmd.clone.sunk | while | flops 271578112 | bytes 5034105 | solution.py:122
  564.3 25.7 %all-gather.4 = f32[8,3,5120]{2,1,0:T(4,128)S(1)} all-gather(f32[1,3,5120]{2,1,0:T(4,128)S(1)} %maximum_bitcast_fusion), channel_id=2, replica_groups=mesh['batch'=2,'items_0'=8,'items_1'=2,'items_2'=4,'items_3'=2] {'items_0'}, dimensions={0}, use_global_device_ids=true | all-gather | bytes 552960 | tf_op jit(solution)/shard_map/all_gather | solution.py:38
  590.7 24.6 %all-gather.5 = f32[2,3,5120]{2,1,0:T(4,128)S(1)} all-gather(f32[1,3,5120]{2,1,0:T(4,128)S(1)} %maximum_bitcast_fusion.1), channel_id=3, replica_groups=mesh['batch'=2,'items_0'=8,'items_1'=2,'items_2'=4,'items_3'=2] {'items_1'}, dimensions={0}, use_global_device_ids=true | all-gather | bytes 184320 | tf_op jit(solution)/shard_map/all_gather | solution.py:38
  615.5 12.4 %all-gather.6 = f32[4,3,5120]{2,1,0:T(4,128)S(1)} all-gather(f32[1,3,5120]{2,1,0:T(4,128)S(1)} %maximum_bitcast_fusion.2), channel_id=4, replica_groups=mesh['batch'=2,'items_0'=8,'items_1'=2,'items_2'=4,'items_3'=2] {'items_2'}, dimensions={0}, use_global_device_ids=true | all-gather | bytes 307200 | tf_op jit(solution)/shard_map/all_gather | solution.py:38
  628.3 1.9 all-gather.7
  630.6 28.3 %while.29 = (s32[]{:T(128)}, f32[512,256]{1,0:T(8,128)}, f32[5,1024,256]{2,1,0:T(8,128)}, bf16[5,1024,256]{2,1,0:T(8,128)(2,1)}, bf16[512,256]{1,0:T(8,128)(2,1)...) while((s32[]{:T(128)}, f32[512,256]{1,0:T(8,128)}, ...), condition=%wide.region_6.7_spmd.clone, body=%wide.region_5.6_spmd.clone.sunk | while | flops 808189952 | bytes 6840451 | solution.py:141
  630.6 1.7 subtract_convert_fusion.2
  632.3 2.4 convolution_add_fusion.2
  636.1 1.7 subtract_convert_fusion.2
  637.9 2.5 convolution_add_fusion.2
  641.9 1.7 subtract_convert_fusion.2
  643.6 2.5 convolution_add_fusion.2
  647.5 1.7 subtract_convert_fusion.2
  649.3 2.5 convolution_add_fusion.2
  653.2 1.7 subtract_convert_fusion.2
  654.9 2.5 convolution_add_fusion.2
  658.9 5.3 copy.7
  664.2 16.3 %reduce-scatter.3.cloned.1.call-done = f32[64,40,256]{2,1,0:T(8,128)} async-done(((f32[128,40,256]{2,1,0:T(8,128)}), f32[64,40,256]{2,1,0:T(8,128)}) %reduce-scatter.3.cloned.1.call-update) | async-done | bytes 2621456 | tf_op jit(solution)/shard_map/reduce_scatter | solution.py:67
  680.6 3.5 all-to-all-start.1
  684.7 9.4 all-to-all-done.1
  694.9 304.3 %reduce-scatter.5.cloned.1.call-done = f32[1,40,256]{2,1,0:T(8,128)} async-done(((f32[64,40,256]{2,1,0:T(8,128)}), f32[1,40,256]{2,1,0:T(8,128)}) %reduce-scatter.5.cloned.1.call-update) | async-done | bytes 40976 | tf_op jit(solution)/shard_map/reduce_scatter | solution.py:68
  (86 shorter events, 25.3 us)
Async XLA Ops:
  7.2 544.6 %all-gather.10.cloned.1.call-start = ((), (), s32[]{:S(2)}) async-start(), calls=%async_computation.4 | async-start | bytes 2641920 | tf_op jit(solution)/shard_map/all_gather | solution.py:95
  9.5 542.3 %all-to-all-start = ((bf16[2,256,256]{2,1,0:T(8,128)(2,1)}), bf16[2,256,256]{2,1,0:T(8,128)(2,1)S(1)}, u32[]{:S(2)}, u32[]{:S(2)}) async-start(bf16[2,256,256]{2,1,0:T(8,128)(2,1)} %broadcast_in_dim.46), calls=%async_computation | async-start | bytes 524288 | tf_op jit(solution)/shard_map/all_to_all | solution.py:21
  13.0 667.6 %reduce-scatter.3.cloned.1.call-start = ((), (), s32[]{:S(2)}) async-start(), calls=%async_computation.5 | async-start | bytes 7864320 | tf_op jit(solution)/shard_map/reduce_scatter | solution.py:67
  664.1 335.1 %reduce-scatter.5.cloned.1.call-start = ((), (), s32[]{:S(2)}) async-start(), calls=%async_computation.6 | async-start | bytes 2662400 | tf_op jit(solution)/shard_map/reduce_scatter | solution.py:68
  680.6 13.6 %all-to-all-start.1 = ((f32[2,256,256]{2,1,0:T(8,128)}), f32[2,256,256]{2,1,0:T(8,128)S(1)}, u32[]{:S(2)}, u32[]{:S(2)}) async-start(f32[2,256,256]{2,1,0:T(8,128)} %bitcast.47), calls=%async_computation.3 | async-start | bytes 1048576 | tf_op jit(solution)/shard_map/all_to_all | solution.py:73
Sparse Core Ops, SparseCore 0:
  9.8 217.5 all-gather.9
  664.3 16.2 reduce-scatter.2
  683.6 315.5 reduce-scatter.4
where the time goes:
time: 1010 us
  blocking collectives  600 us (59%)
  waiting for transfers between devices  331 us (33%)
  matrix products  35.7 us (4%)
  between operations  14.7 us (1%)
  local copies, waits for them, and re-layouts  10.9 us (1%)
    unnamed x1, blocking collectives  536 us
    reduce_scatter x1, waiting for transfers between devices, summed_rows(): return lax.psum_scatter(blocks, chips, scatter_dimension=0, tiled=True)[0]  304 us
    all_gather x4, blocking collectives, all_in_one(): both, at, found = (lax.all_gather(jnp.concatenate(lines), axis), 0, {})  64.7 us
  transfers between devices with their start and end apart: 5, of which 3 were waited for; matrix products, arithmetic and copies ran while one was open for 1% of the time, Pallas kernels for 0%

commit v1 on v0

v1 whole, which is shorter than its diff:
```python
import jax
import jax.numpy as jnp
from jax import lax
from jax.experimental import pallas as pl
from jax.experimental.pallas import tpu as pltpu
from jax.sharding import Mesh
from jax.sharding import PartitionSpec as P

AXES = ("xh", "z", "xl", "y", "c")
MESH = pl.DeviceIdType.MESH
F32 = jnp.float32
BF16 = jnp.bfloat16
NX, NY, NZ, NC = 4, 4, 8, 2
OWN = 40
ROW = 48
ITM = 256
E = 256
CH = NZ * ROW


def kernel(blk, items, loss_out, ug_out, ig_out, U, I, IT, HL, LG, EX, MB, SB, PB, W, ST, PT, YST, YPT, ZST, ZPT, SC,
           UG, YR2, YR1, ZR, G, PG, XR2, XR1,
           s_send, s_u, s_i, s_ys, s_yp, s_zs, s_zp, s_y2, s_y1, s_zr, s_pg, s_x2, s_x1):
    xh, z, xl, y, c = (lax.axis_index(a) for a in AXES)
    x = 2 * xh + xl

    def dev(dx=0, dy=0, dz=0, dc=0):
        nx = lax.rem(x + dx, NX)
        nc = lax.rem(c + dc, NC)
        return (nx // 2, lax.rem(z + dz, NZ), lax.rem(nx, 2), lax.rem(y + dy, NY), nc)

    sent = []

    def send(src, dst, recv, where):
        copy = pltpu.make_async_remote_copy(
            src_ref=src, dst_ref=dst, send_sem=s_send.at[len(sent)], recv_sem=recv,
            device_id=where, device_id_type=MESH,
        )
        copy.start()
        sent.append(copy)

    def arrived(dst, recv):
        pltpu.make_async_remote_copy(
            src_ref=dst, dst_ref=dst, send_sem=s_send.at[0], recv_sem=recv,
            device_id=dev(dc=1), device_id_type=MESH,
        ).wait_recv()

    yy = [lax.rem(y + d, NY) for d in range(NY)]
    zz = [lax.rem(z + d, NZ) for d in range(NZ)]
    xx = [lax.rem(x + d, NX) for d in range(NX)]
    co = 1 - c

    barrier = pltpu.get_barrier_semaphore()
    peers = [dict(dz=d) for d in range(1, NZ)] + [dict(dy=d) for d in range(1, NY)]
    peers += [dict(dx=1), dict(dx=3), dict(dc=1)]
    for p in peers:
        pl.semaphore_signal(barrier, inc=1, device_id=dev(**p), device_id_type=MESH)

    U[y * NZ + z] = blk[...]
    I[x * NC + c] = items[...]
    pl.semaphore_wait(barrier, len(peers))

    H = ITM // 2
    bo = x * NC + c

    def halves(b, order=(0, 1)):
        return [(h, I.at[b, pl.ds(h * H, H)], s_i.at[2 * b + h]) for h in order]

    mine = y * NZ + z
    for d in (1, 7, 2, 6, 3, 5, 4):
        send(blk, U.at[mine], s_u.at[mine], dev(dz=d))
    for d in (1, 3):
        send(blk, U.at[mine], s_u.at[mine], dev(dy=d))
    for dx, order in ((1, (0, 1)), (3, (1, 0))):
        for h, dst, sem in halves(bo, order):
            send(items.at[pl.ds(h * H, H)], dst, sem, dev(dx=dx))
    for h, dst, sem in halves(bo):
        send(items.at[pl.ds(h * H, H)], dst, sem, dev(dc=1))

    for d in (1, 7, 2, 6, 3, 5, 4):
        s = y * NZ + zz[d]
        arrived(U.at[s], s_u.at[s])
        for dy in (1, 3):
            send(U.at[s], U.at[s], s_u.at[s], dev(dy=dy))

    for dx, keep in ((3, 0), (1, 1)):
        b = xx[dx] * NC + c
        for h, ref, sem in halves(b, (keep, 1 - keep)):
            arrived(ref, sem)
            if h == keep:
                send(ref, ref, sem, dev(dx=4 - dx))
            send(ref, ref, sem, dev(dc=1))

    def place_ids(yi):
        part = U[pl.ds(yi * NZ, NZ), OWN:ROW, 0:128].astype(F32)
        n = lax.broadcasted_iota(jnp.int32, (128, CH), 1)
        k = (n * 1366) >> 16
        pick = jnp.where(n - k * ROW == lax.broadcasted_iota(jnp.int32, (128, CH), 0), 1.0, 0.0)
        pick = pick.astype(BF16)
        n8 = lax.broadcasted_iota(jnp.int32, (NZ, CH), 1)
        k8 = (n8 * 1366) >> 16
        here = k8 == lax.broadcasted_iota(jnp.int32, (NZ, CH), 0)
        for j in range(2):
            spread = jnp.dot(part[:, j, :].astype(BF16), pick, preferred_element_type=F32)
            HL[yi, j] = jnp.sum(jnp.where(here, spread, 0.0), axis=0, keepdims=True)

    n1 = lax.broadcasted_iota(jnp.int32, (1, CH), 1)
    valid = n1 - ((n1 * 1366) >> 16) * ROW < OWN

    def target(yi, bx, bc):
        owner = (bx // 2) * 128 + z * 16 + lax.rem(bx, 2) * 8 + y * 2 + bc
        match = (HL[yi, 0] == owner.astype(F32)) & valid
        return jnp.where(match, HL[yi, 1], -1.0)

    rows = lax.broadcasted_iota(jnp.int32, (ITM, 128), 0).astype(F32)

    def first(yi, bx, bc):
        b = bx * NC + bc
        users = U[pl.ds(yi * NZ, NZ)].reshape(CH, E)
        LG[...] = lax.dot_general(I[b], users, (((1,), (1,)), ((), ())), preferred_element_type=F32)
        at = target(yi, bx, bc)
        for j in range(CH // 128):
            cols = slice(128 * j, 128 * j + 128)
            lg = LG[:, cols]
            top = jnp.max(lg, axis=0, keepdims=True)
            ex = jnp.exp(lg - top)
            EX[b, yi, :, cols] = ex
            MB[yi, b, :, cols] = top
            SB[yi, b, :, cols] = jnp.sum(ex, axis=0, keepdims=True)
            PB[yi, b, :, cols] = jnp.sum(jnp.where(rows == at[:, cols], lg, 0.0), axis=0, keepdims=True)

    def turn(b):
        IT[b] = I[b].T

    place_ids(yy[0])
    for dx in (0, 3, 1):
        first(yy[0], xx[dx], c)
        turn(xx[dx] * NC + c)

    for dy, first_z in ((3, 0), (1, 1)):
        for d in range(NZ):
            s = yy[dy] * NZ + d
            arrived(U.at[s], s_u.at[s])
            if (d < NZ // 2) == (first_z == 0):
                send(U.at[s], U.at[s], s_u.at[s], dev(dy=4 - dy))

    b = xx[2] * NC + c
    for h, ref, sem in halves(b):
        arrived(ref, sem)
        send(ref, ref, sem, dev(dc=1))
    first(yy[0], xx[2], c)
    turn(b)
    for dx in (0, 3, 1, 2):
        b = xx[dx] * NC + co
        for h, ref, sem in halves(b):
            arrived(ref, sem)
        first(yy[0], xx[dx], co)
        turn(b)

    for dy in (3, 1):
        place_ids(yy[dy])
        lax.fori_loop(0, NX * NC, lambda i, _: (first(yy[dy], i // NC, lax.rem(i, NC)), 0)[1], 0)
    for d in range(NZ):
        s = yy[2] * NZ + d
        arrived(U.at[s], s_u.at[s])
    place_ids(yy[2])
    lax.fori_loop(0, NX * NC, lambda i, _: (first(yy[2], i // NC, lax.rem(i, NC)), 0)[1], 0)

    NR = CH // 128
    for k in range(NY):
        m = jnp.max(MB[k], axis=0)
        s = jnp.sum(SB[k] * jnp.exp(MB[k] - m[None]), axis=0)
        p = jnp.sum(PB[k], axis=0)
        for j in range(NR):
            cols = slice(128 * j, 128 * j + 128)
            r = NR * k + j
            ST[r : r + 1] = m[:, cols]
            ST[12 + r : 13 + r] = s[:, cols]
            PT[r : r + 1] = p[:, cols]
    PT[12:16] = jnp.zeros((4, 128), F32)

    def combine(parts):
        m = parts[0][0:12]
        for q in parts[1:]:
            m = jnp.maximum(m, q[0:12])
        s = jnp.zeros_like(m)
        for q in parts:
            s = s + q[12:24] * jnp.exp(q[0:12] - m)
        return m, s

    for d in (1, 3, 2):
        send(ST, YST.at[y], s_ys.at[y], dev(dy=d))
    for d in (1, 3, 2):
        send(PT, YPT.at[y], s_yp.at[y], dev(dy=d))
    for d in (1, 3, 2):
        arrived(YST.at[yy[d]], s_ys.at[yy[d]])
    YST[y] = ST[...]
    m, s = combine([YST[k] for k in range(NY)])
    ZST[z, 0:12] = m
    ZST[z, 12:24] = s
    for d in (4, 3, 5, 2, 6, 1, 7):
        send(ZST.at[z], ZST.at[z], s_zs.at[z], dev(dz=d))
    for d in (1, 3, 2):
        arrived(YPT.at[yy[d]], s_yp.at[yy[d]])
    YPT[y] = PT[...]
    ZPT[z] = (YPT[0] + YPT[1]) + (YPT[2] + YPT[3])
    for d in (4, 3, 5, 2, 6, 1, 7):
        send(ZPT.at[z], ZPT.at[z], s_zp.at[z], dev(dz=d))
    for d in (1, 7, 2, 6, 3, 5, 4):
        arrived(ZST.at[zz[d]], s_zs.at[zz[d]])
    m, s = combine([ZST[k] for k in range(NZ)])
    lse = m + jnp.log(s)
    for k in range(NY):
        for j in range(NR):
            r = NR * k + j
            SC[k, :, 128 * j : 128 * j + 128] = lse[r : r + 1]

    def second(yi, bx, bc):
        b = bx * NC + bc
        at = target(yi, bx, bc)
        scale = jnp.where(valid, jnp.exp(MB[yi, b] - SC[yi]), 0.0)
        for j in range(CH // 128):
            cols = slice(128 * j, 128 * j + 128)
            w = EX[b, yi, :, cols] * scale[:, cols]
            w = w - jnp.where(rows == at[:, cols], 1.0, 0.0)
            W[b, yi, :, cols] = w.astype(BF16)

    def user_terms(d):
        yi = yy[d]
        lax.fori_loop(0, NX * NC, lambda i, _: (second(yi, i // NC, lax.rem(i, NC)), 0)[1], 0)
        acc = jnp.dot(IT[0], W[0, yi], preferred_element_type=F32)
        for b in range(1, NX * NC):
            acc += jnp.dot(IT[b], W[b, yi], preferred_element_type=F32)
        UG[d] = acc.T.reshape(NZ, ROW, E)

    HZ = NZ // 2
    user_terms(2)
    lo, hi = pl.ds(0, HZ), pl.ds(HZ, HZ)
    own = pl.ds(0, OWN)
    send(UG.at[2, lo, own], YR2.at[0], s_y2.at[0], dev(dy=1))
    send(UG.at[2, hi, own], YR2.at[1], s_y2.at[1], dev(dy=3))
    user_terms(1)
    send(UG.at[1, hi, own], YR1.at[0, hi], s_y1.at[1], dev(dy=1))
    user_terms(3)
    send(UG.at[3, lo, own], YR1.at[1, lo], s_y1.at[2], dev(dy=3))
    user_terms(0)

    def item_terms(b):
        acc = jnp.dot(W[b, 0], U[0:NZ].reshape(CH, E), preferred_element_type=F32)
        for k in range(1, NY):
            acc += jnp.dot(W[b, k], U[k * NZ : k * NZ + NZ].reshape(CH, E), preferred_element_type=F32)
        G[b] = acc

    for dx in (2, 1):
        b = xx[dx] * NC + co
        item_terms(b)
        send(G.at[b], PG.at[xx[dx]], s_pg.at[xx[dx]], dev(dc=1))
    arrived(YR2.at[0], s_y2.at[0])
    UG[1, 0:HZ, 0:OWN] += YR2[0]
    send(UG.at[1, lo, own], YR1.at[0, lo], s_y1.at[0], dev(dy=1))
    arrived(YR2.at[1], s_y2.at[1])
    UG[3, HZ:NZ, 0:OWN] += YR2[1]
    send(UG.at[3, hi, own], YR1.at[1, hi], s_y1.at[3], dev(dy=3))
    for dx in (3, 0):
        b = xx[dx] * NC + co
        item_terms(b)
        send(G.at[b], PG.at[xx[dx]], s_pg.at[xx[dx]], dev(dc=1))

    def own_terms(dx):
        b = xx[dx] * NC + c
        item_terms(b)
        arrived(PG.at[xx[dx]], s_pg.at[xx[dx]])
        G[b] += PG[xx[dx]]
        return b

    top, bot = pl.ds(0, H), pl.ds(H, H)
    b = own_terms(2)
    send(G.at[b, top], XR2.at[0], s_x2.at[0], dev(dx=1))
    send(G.at[b, bot], XR2.at[1], s_x2.at[1], dev(dx=3))
    b1 = own_terms(1)
    send(G.at[b1, bot], XR1.at[0, bot], s_x1.at[1], dev(dx=1))
    b3 = own_terms(3)
    send(G.at[b3, top], XR1.at[1, top], s_x1.at[2], dev(dx=3))

    for i, part in ((1, hi), (2, lo), (0, lo), (3, hi)):
        arrived(YR1.at[i // 2, part], s_y1.at[i])
    UG[0, :, 0:OWN] = UG[0, :, 0:OWN] + YR1[0] + YR1[1]
    for d in (4, 3, 5, 2, 6, 1, 7):
        send(UG.at[0, zz[d], own], ZR.at[z], s_zr.at[z], dev(dz=d))

    b0 = own_terms(0)
    arrived(XR2.at[0], s_x2.at[0])
    G[b1, 0:H] += XR2[0]
    send(G.at[b1, top], XR1.at[0, top], s_x1.at[0], dev(dx=1))
    arrived(XR2.at[1], s_x2.at[1])
    G[b3, H:ITM] += XR2[1]
    send(G.at[b3, bot], XR1.at[1, bot], s_x1.at[3], dev(dx=3))

    for d in (1, 7, 2, 6, 3, 5, 4):
        arrived(ZPT.at[zz[d]], s_zp.at[zz[d]])
    pos = ZPT[0]
    for k in range(1, NZ):
        pos = pos + ZPT[k]
    for k in range(NY):
        for j in range(NR):
            r = NR * k + j
            PB[k, 0, :, 128 * j : 128 * j + 128] = lse[r : r + 1] - pos[r : r + 1]
    line = PB[y, 0]
    out = line[:, 0:ROW]
    for k in range(1, NZ):
        out = jnp.where(z == k, line[:, ROW * k : ROW * k + ROW], out)
    loss_out[:, 0:ROW] = out
    loss_out[:, ROW:128] = jnp.zeros((1, 128 - ROW), F32)

    total = UG[0, z, 0:OWN]
    for d in range(1, NZ):
        arrived(ZR.at[zz[d]], s_zr.at[zz[d]])
        total = total + ZR[zz[d]]
    ug_out[...] = total

    for i, part in ((1, bot), (2, top), (0, top), (3, bot)):
        arrived(XR1.at[i // 2, part], s_x1.at[i])
    ig_out[...] = G[b0] + XR1[0] + XR1[1]

    for copy in sent:
        copy.wait_send()


def local(users, items, pos_ids):
    ids = jnp.stack([pos_ids >> 8, pos_ids & 255]).astype(BF16)
    ids = jnp.pad(ids, ((0, ROW - OWN - 2), (0, E - OWN)))
    blk = jnp.concatenate([users, ids], axis=0)
    V = pltpu.VMEM
    D = pltpu.SemaphoreType.DMA
    scratch = [
        V((NY * NZ, ROW, E), BF16),
        V((NX * NC, ITM, E), BF16),
        V((NX * NC, E, ITM), BF16),
        V((NY, 2, 1, CH), F32),
        V((ITM, CH), F32),
        V((NX * NC, NY, ITM, CH), F32),
        V((NY, NX * NC, 1, CH), F32),
        V((NY, NX * NC, 1, CH), F32),
        V((NY, NX * NC, 1, CH), F32),
        V((NX * NC, NY, ITM, CH), BF16),
        V((24, 128), F32),
        V((16, 128), F32),
        V((NY, 24, 128), F32),
        V((NY, 16, 128), F32),
        V((NZ, 24, 128), F32),
        V((NZ, 16, 128), F32),
        V((NY, 1, CH), F32),
        V((NY, NZ, ROW, E), F32),
        V((2, NZ // 2, OWN, E), F32),
        V((2, NZ, OWN, E), F32),
        V((NZ, OWN, E), F32),
        V((NX * NC, ITM, E), F32),
        V((NX, ITM, E), F32),
        V((2, ITM // 2, E), F32),
        V((2, ITM, E), F32),
        D((128,)),
        D((NY * NZ,)),
        D((2 * NX * NC,)),
        D((NY,)), D((NY,)), D((NZ,)), D((NZ,)),
        D((2,)), D((4,)), D((NZ,)), D((NX,)), D((2,)), D((4,)),
    ]
    loss, ug, ig = pl.pallas_call(
        kernel,
        out_shape=(
            jax.ShapeDtypeStruct((1, 128), F32),
            jax.ShapeDtypeStruct((OWN, E), F32),
            jax.ShapeDtypeStruct((ITM, E), F32),
        ),
        in_specs=[pl.BlockSpec(memory_space=pltpu.VMEM)] * 2,
        out_specs=tuple([pl.BlockSpec(memory_space=pltpu.VMEM)] * 3),
        scratch_shapes=scratch,
        compiler_params=pltpu.CompilerParams(
            collective_id=0, has_side_effects=True, vmem_limit_bytes=60 * 2**20
        ),
        name="infonce",
    )(blk, items)
    return loss[0, :OWN], ug, ig


def solution(mesh):
    torus = Mesh(mesh.devices.reshape(2, NZ, 2, NY, NC), AXES)
    every = P(AXES)
    return jax.shard_map(
        local,
        mesh=torus,
        in_specs=(P(AXES, None), P(AXES, None), every),
        out_specs=(every, P(AXES, None), P(AXES, None)),
        check_vma=False,
    )
```

time: 1010 us -> 71 us (0.07)
  the two profiles are of different devices: /device:TPU:2 before, /device:TPU:1 now
where the time goes in v1:
time: 71 us; the launch traced here: 70.7 us
  Pallas kernels  63.9 us (90%)
  local copies, waits for them, and re-layouts  4.18 us (6%)
  other arithmetic  2.01 us (3%)
    pallas_call x1, Pallas kernels, local(): pl.pallas_call(kernel, out_shape=(jax.ShapeDtypeStruct((1, 128), F32), ja...  63.9 us
    unnamed x4, local copies, waits for them, and re-layouts  3.67 us

profile of v1, /device:TPU:1, one launch (start us, length us, event | category | flops | bytes accessed | tf_op | source)
XLA Modules:
  0.0 70.7 jit_solution(513646813116212079)
XLA Ops:
  0.6 0.7 convert_bitcast_fusion.1
  1.3 1.3 %pad_maximum_fusion.blk = bf16[48,256]{1,0:T(8,128)(2,1)} fusion(bf16[8,256]{1,0:T(8,128)(2,1)S(1)} %fusion.5, bf16[40,256]{1,0:T(8,128)(2,1)} %param.3), kind=kLoop, calls=%fused_computation | loop fusion | flops 49152 | bytes 49152 | tf_op jit(solution)/shard_map/concatenate | solution.py:332
  2.6 63.9 %infonce.1 = (f32[1,128]{1,0:T(1,128)}, f32[40,256]{1,0:T(8,128)}, f32[256,256]{1,0:T(8,128)}) custom-call(bf16[48,256]{1,0:T(8,128)(2,1)} %pad_maximum_fusion.blk, bf16[256,256]{1,0:T(8,128)(2,1)} %items.1), custom_call_target="tpu_custom_call" | custom-call | tf_op jit(solution)/shard_map/infonce/pallas_call | solution.py:367
  66.5 0.0 copy-start
  66.6 0.6 copy-done
  67.2 0.5 slice_bitcast_fusion
  67.7 1.4 %copy.8 = f32[40,256]{1,0:T(8,128)} copy(f32[40,256]{1,0:T(8,128)} %get-tuple-element.15) | data formatting | bytes 81920
  69.1 1.7 %copy.9 = f32[256,256]{1,0:T(8,128)} copy(f32[256,256]{1,0:T(8,128)} %get-tuple-element.16) | data formatting | bytes 524288
  (1 shorter events, 0.0 us)
Async XLA Ops:
  66.5 0.6 copy-start

commit v2 on v1

--- a/solution.py
+++ b/solution.py
@@ -18,9 +18,25 @@
 CH = NZ * ROW
 
 
-def kernel(blk, items, loss_out, ug_out, ig_out, U, I, IT, HL, LG, EX, MB, SB, PB, W, ST, PT, YST, YPT, ZST, ZPT, SC,
-           UG, YR2, YR1, ZR, G, PG, XR2, XR1,
-           s_send, s_u, s_i, s_ys, s_yp, s_zs, s_zp, s_y2, s_y1, s_zr, s_pg, s_x2, s_x1):
+TOP = 32704.0
+
+
+def code(v, q, m):
+    for j in range(v.shape[1] // 128):
+        cols = slice(128 * j, 128 * j + 128)
+        part = v[:, cols]
+        most = jnp.maximum(jnp.max(jnp.abs(part), axis=0, keepdims=True), 1e-30)
+        m[:, cols] = most
+        q[:, cols] = jnp.round(part * (TOP / most)).astype(jnp.int16)
+
+
+def decode(q, m):
+    return q.astype(F32) * (m * (1.0 / TOP))
+
+
+def kernel(users, items, ids, loss_out, ug_out, ig_out, U, I, ID, IT, UT, HL, LG, EX, MB, SB, PB, W, ST, PT, YST, YPT, ZST, ZPT,
+           SC, UG, UZ, QY2, MY2, QY1, MY1, YQ2, YM2, YQ1, YM1, QZ, MZ, ZQ, ZM, G, QP, MP, PQ, PM, QX2, MX2, QX1, MX1, XQ2, XM2,
+           XQ1, XM1, s_in, s_send, s_u, s_i, s_ys, s_yp, s_zs, s_zp, s_y2, s_y1, s_zr, s_pg, s_x2, s_x1):
     xh, z, xl, y, c = (lax.axis_index(a) for a in AXES)
     x = 2 * xh + xl
 
@@ -50,32 +66,46 @@
     xx = [lax.rem(x + d, NX) for d in range(NX)]
     co = 1 - c
 
+    mine = y * NZ + z
+    bo = x * NC + c
+    inputs = [
+        pltpu.make_async_copy(users, U.at[mine, pl.ds(0, OWN)], s_in.at[0]),
+        pltpu.make_async_copy(items, I.at[bo], s_in.at[1]),
+        pltpu.make_async_copy(ids, ID, s_in.at[2]),
+    ]
+    for copy in inputs:
+        copy.start()
     barrier = pltpu.get_barrier_semaphore()
     peers = [dict(dz=d) for d in range(1, NZ)] + [dict(dy=d) for d in range(1, NY)]
     peers += [dict(dx=1), dict(dx=3), dict(dc=1)]
     for p in peers:
         pl.semaphore_signal(barrier, inc=1, device_id=dev(**p), device_id_type=MESH)
 
-    U[y * NZ + z] = blk[...]
-    I[x * NC + c] = items[...]
+    for copy in inputs:
+        copy.wait()
+    PB[0, 0] = jnp.zeros((1, CH), F32)
+    PB[1, 0] = jnp.zeros((1, CH), F32)
+    PB[0, 0, :, 0:OWN] = (ID[...] >> 8).astype(F32)
+    PB[1, 0, :, 0:OWN] = (ID[...] & 255).astype(F32)
+    r8 = lax.broadcasted_iota(jnp.int32, (ROW - OWN, E), 0)
+    pad = jnp.where(r8 == 0, PB[0, 0, :, 0:E], jnp.where(r8 == 1, PB[1, 0, :, 0:E], 0.0))
+    U[mine, OWN:ROW] = pad.astype(BF16)
     pl.semaphore_wait(barrier, len(peers))
 
     H = ITM // 2
-    bo = x * NC + c
 
     def halves(b, order=(0, 1)):
         return [(h, I.at[b, pl.ds(h * H, H)], s_i.at[2 * b + h]) for h in order]
 
-    mine = y * NZ + z
     for d in (1, 7, 2, 6, 3, 5, 4):
-        send(blk, U.at[mine], s_u.at[mine], dev(dz=d))
+        send(U.at[mine], U.at[mine], s_u.at[mine], dev(dz=d))
     for d in (1, 3):
-        send(blk, U.at[mine], s_u.at[mine], dev(dy=d))
+        send(U.at[mine], U.at[mine], s_u.at[mine], dev(dy=d))
     for dx, order in ((1, (0, 1)), (3, (1, 0))):
         for h, dst, sem in halves(bo, order):
-            send(items.at[pl.ds(h * H, H)], dst, sem, dev(dx=dx))
+            send(dst, dst, sem, dev(dx=dx))
     for h, dst, sem in halves(bo):
-        send(items.at[pl.ds(h * H, H)], dst, sem, dev(dc=1))
+        send(dst, dst, sem, dev(dc=1))
 
     for d in (1, 7, 2, 6, 3, 5, 4):
         s = y * NZ + zz[d]
@@ -92,6 +122,7 @@
             send(ref, ref, sem, dev(dc=1))
 
     def place_ids(yi):
+        UT[yi] = U[pl.ds(yi * NZ, NZ)].reshape(CH, E).T
         part = U[pl.ds(yi * NZ, NZ), OWN:ROW, 0:128].astype(F32)
         n = lax.broadcasted_iota(jnp.int32, (128, CH), 1)
         k = (n * 1366) >> 16
@@ -116,8 +147,7 @@
 
     def first(yi, bx, bc):
         b = bx * NC + bc
-        users = U[pl.ds(yi * NZ, NZ)].reshape(CH, E)
-        LG[...] = lax.dot_general(I[b], users, (((1,), (1,)), ((), ())), preferred_element_type=F32)
+        LG[...] = jnp.dot(I[b], UT[yi], preferred_element_type=F32)
         at = target(yi, bx, bc)
         for j in range(CH // 128):
             cols = slice(128 * j, 128 * j + 128)
@@ -231,18 +261,43 @@
         acc = jnp.dot(IT[0], W[0, yi], preferred_element_type=F32)
         for b in range(1, NX * NC):
             acc += jnp.dot(IT[b], W[b, yi], preferred_element_type=F32)
-        UG[d] = acc.T.reshape(NZ, ROW, E)
-
-    HZ = NZ // 2
+        UG[d] = acc
+
+    H = E // 2
+    half = [pl.ds(0, H), pl.ds(H, H)]
+
+    def send2(q, qto, m, mto, recv, i, where):
+        send(q, qto, recv.at[i, 0], where)
+        send(m, mto, recv.at[i, 1], where)
+
+    def arrived2(q, m, recv, i):
+        arrived(q, recv.at[i, 0])
+        arrived(m, recv.at[i, 1])
+
     user_terms(2)
-    lo, hi = pl.ds(0, HZ), pl.ds(HZ, HZ)
-    own = pl.ds(0, OWN)
-    send(UG.at[2, lo, own], YR2.at[0], s_y2.at[0], dev(dy=1))
-    send(UG.at[2, hi, own], YR2.at[1], s_y2.at[1], dev(dy=3))
+    for i in range(2):
+        code(UG[2, H * i : H * i + H], QY2.at[i], MY2.at[i])
+        send2(QY2.at[i], YQ2.at[i], MY2.at[i], YM2.at[i], s_y2, i, dev(dy=1 + 2 * i))
+
+    def direct(d, i):
+        h = 1 - i
+        k = 2 * i + h
+        code(UG[d, H * h : H * h + H], QY1.at[k], MY1.at[k])
+        send2(QY1.at[k], YQ1.at[k], MY1.at[k], YM1.at[k], s_y1, k, dev(dy=d))
+
+    def relayed(d, i):
+        h = i
+        k = 2 * i + h
+        arrived2(YQ2.at[i], YM2.at[i], s_y2, i)
+        code(UG[d, H * h : H * h + H] + decode(YQ2[i], YM2[i]), QY1.at[k], MY1.at[k])
+        send2(QY1.at[k], YQ1.at[k], MY1.at[k], YM1.at[k], s_y1, k, dev(dy=d))
+
     user_terms(1)
-    send(UG.at[1, hi, own], YR1.at[0, hi], s_y1.at[1], dev(dy=1))
+    direct(1, 0)
     user_terms(3)
-    send(UG.at[3, lo, own], YR1.at[1, lo], s_y1.at[2], dev(dy=3))
+    direct(3, 1)
+    relayed(1, 0)
+    relayed(3, 1)
     user_terms(0)
 
     def item_terms(b):
@@ -251,50 +306,57 @@
             acc += jnp.dot(W[b, k], U[k * NZ : k * NZ + NZ].reshape(CH, E), preferred_element_type=F32)
         G[b] = acc
 
-    for dx in (2, 1):
+    for dx in (2, 1, 3, 0):
         b = xx[dx] * NC + co
         item_terms(b)
-        send(G.at[b], PG.at[xx[dx]], s_pg.at[xx[dx]], dev(dc=1))
-    arrived(YR2.at[0], s_y2.at[0])
-    UG[1, 0:HZ, 0:OWN] += YR2[0]
-    send(UG.at[1, lo, own], YR1.at[0, lo], s_y1.at[0], dev(dy=1))
-    arrived(YR2.at[1], s_y2.at[1])
-    UG[3, HZ:NZ, 0:OWN] += YR2[1]
-    send(UG.at[3, hi, own], YR1.at[1, hi], s_y1.at[3], dev(dy=3))
-    for dx in (3, 0):
-        b = xx[dx] * NC + co
-        item_terms(b)
-        send(G.at[b], PG.at[xx[dx]], s_pg.at[xx[dx]], dev(dc=1))
+        code(G[b], QP.at[dx], MP.at[dx])
+        send2(QP.at[dx], PQ.at[dx], MP.at[dx], PM.at[dx], s_pg, dx, dev(dc=1))
+
+    total = []
+    for h in range(2):
+        v = UG[0, H * h : H * h + H]
+        for i in range(2):
+            k = 2 * i + h
+            arrived2(YQ1.at[k], YM1.at[k], s_y1, k)
+            v = v + decode(YQ1[k], YM1[k])
+        UG[0, H * h : H * h + H] = v
+    UZ[...] = UG[0].T.reshape(NZ, ROW, E)
+    for d in (4, 3, 5, 2, 6, 1, 7):
+        code(UZ[zz[d], 0:OWN], QZ.at[d], MZ.at[d])
+        send2(QZ.at[d], ZQ.at[d], MZ.at[d], ZM.at[d], s_zr, d, dev(dz=d))
 
     def own_terms(dx):
         b = xx[dx] * NC + c
         item_terms(b)
-        arrived(PG.at[xx[dx]], s_pg.at[xx[dx]])
-        G[b] += PG[xx[dx]]
+        arrived2(PQ.at[dx], PM.at[dx], s_pg, dx)
+        G[b] += decode(PQ[dx], PM[dx])
         return b
 
-    top, bot = pl.ds(0, H), pl.ds(H, H)
-    b = own_terms(2)
-    send(G.at[b, top], XR2.at[0], s_x2.at[0], dev(dx=1))
-    send(G.at[b, bot], XR2.at[1], s_x2.at[1], dev(dx=3))
-    b1 = own_terms(1)
-    send(G.at[b1, bot], XR1.at[0, bot], s_x1.at[1], dev(dx=1))
-    b3 = own_terms(3)
-    send(G.at[b3, top], XR1.at[1, top], s_x1.at[2], dev(dx=3))
-
-    for i, part in ((1, hi), (2, lo), (0, lo), (3, hi)):
-        arrived(YR1.at[i // 2, part], s_y1.at[i])
-    UG[0, :, 0:OWN] = UG[0, :, 0:OWN] + YR1[0] + YR1[1]
-    for d in (4, 3, 5, 2, 6, 1, 7):
-        send(UG.at[0, zz[d], own], ZR.at[z], s_zr.at[z], dev(dz=d))
-
+    b2 = own_terms(2)
+    for i in range(2):
+        code(G[b2, H * i : H * i + H], QX2.at[i], MX2.at[i])
+        send2(QX2.at[i], XQ2.at[i], MX2.at[i], XM2.at[i], s_x2, i, dev(dx=1 + 2 * i))
+
+    def x_direct(dx, i):
+        b = own_terms(dx)
+        h = 1 - i
+        k = 2 * i + h
+        code(G[b, H * h : H * h + H], QX1.at[k], MX1.at[k])
+        send2(QX1.at[k], XQ1.at[k], MX1.at[k], XM1.at[k], s_x1, k, dev(dx=dx))
+        return b
+
+    def x_relayed(b, dx, i):
+        h = i
+        k = 2 * i + h
+        arrived2(XQ2.at[i], XM2.at[i], s_x2, i)
+        code(G[b, H * h : H * h + H] + decode(XQ2[i], XM2[i]), QX1.at[k], MX1.at[k])
+        send2(QX1.at[k], XQ1.at[k], MX1.at[k], XM1.at[k], s_x1, k, dev(dx=dx))
+
+    b1 = x_direct(1, 0)
+    b3 = x_direct(3, 1)
+    x_relayed(b1, 1, 0)
+    x_relayed(b3, 3, 1)
     b0 = own_terms(0)
-    arrived(XR2.at[0], s_x2.at[0])
-    G[b1, 0:H] += XR2[0]
-    send(G.at[b1, top], XR1.at[0, top], s_x1.at[0], dev(dx=1))
-    arrived(XR2.at[1], s_x2.at[1])
-    G[b3, H:ITM] += XR2[1]
-    send(G.at[b3, bot], XR1.at[1, bot], s_x1.at[3], dev(dx=3))
 
     for d in (1, 7, 2, 6, 3, 5, 4):
         arrived(ZPT.at[zz[d]], s_zp.at[zz[d]])
@@ -312,30 +374,53 @@
     loss_out[:, 0:ROW] = out
     loss_out[:, ROW:128] = jnp.zeros((1, 128 - ROW), F32)
 
-    total = UG[0, z, 0:OWN]
-    for d in range(1, NZ):
-        arrived(ZR.at[zz[d]], s_zr.at[zz[d]])
-        total = total + ZR[zz[d]]
+    total = UZ[z, 0:OWN]
+    for d in (1, 7, 2, 6, 3, 5, 4):
+        arrived2(ZQ.at[d], ZM.at[d], s_zr, d)
+        total = total + decode(ZQ[d], ZM[d])
     ug_out[...] = total
 
-    for i, part in ((1, bot), (2, top), (0, top), (3, bot)):
-        arrived(XR1.at[i // 2, part], s_x1.at[i])
-    ig_out[...] = G[b0] + XR1[0] + XR1[1]
+    for h in range(2):
+        v = G[b0, H * h : H * h + H]
+        for i in range(2):
+            k = 2 * i + h
+            arrived2(XQ1.at[k], XM1.at[k], s_x1, k)
+            v = v + decode(XQ1[k], XM1[k])
+        ig_out[H * h : H * h + H] = v
 
     for copy in sent:
         copy.wait_send()
 
 
+def finish(loss, ug, ig, loss_out, ug_out, ig_out, vl, vu, vi, sem):
+    into = [
+        pltpu.make_async_copy(a, b, sem.at[k])
+        for k, (a, b) in enumerate(((ig, vi), (ug, vu), (loss, vl)))
+    ]
+    out = [
+        pltpu.make_async_copy(a, b, sem.at[k + 3])
+        for k, (a, b) in enumerate(((vi, ig_out), (vu, ug_out), (vl, loss_out)))
+    ]
+    for copy in into:
+        copy.start()
+    for a, b in zip(into, out):
+        a.wait()
+        b.start()
+    for copy in out:
+        copy.wait()
+
+
 def local(users, items, pos_ids):
-    ids = jnp.stack([pos_ids >> 8, pos_ids & 255]).astype(BF16)
-    ids = jnp.pad(ids, ((0, ROW - OWN - 2), (0, E - OWN)))
-    blk = jnp.concatenate([users, ids], axis=0)
     V = pltpu.VMEM
     D = pltpu.SemaphoreType.DMA
+    I16 = jnp.int16
+    HE = E // 2
     scratch = [
         V((NY * NZ, ROW, E), BF16),
         V((NX * NC, ITM, E), BF16),
+        V((1, OWN), jnp.int32),
         V((NX * NC, E, ITM), BF16),
+        V((NY, E, CH), BF16),
         V((NY, 2, 1, CH), F32),
         V((ITM, CH), F32),
         V((NX * NC, NY, ITM, CH), F32),
@@ -350,35 +435,53 @@
         V((NZ, 24, 128), F32),
         V((NZ, 16, 128), F32),
         V((NY, 1, CH), F32),
-        V((NY, NZ, ROW, E), F32),
-        V((2, NZ // 2, OWN, E), F32),
-        V((2, NZ, OWN, E), F32),
-        V((NZ, OWN, E), F32),
+        V((NY, E, CH), F32),
+        V((NZ, ROW, E), F32),
+        V((2, HE, CH), I16), V((2, 1, CH), F32),
+        V((4, HE, CH), I16), V((4, 1, CH), F32),
+        V((2, HE, CH), I16), V((2, 1, CH), F32),
+        V((4, HE, CH), I16), V((4, 1, CH), F32),
+        V((NZ, OWN, E), I16), V((NZ, 1, E), F32),
+        V((NZ, OWN, E), I16), V((NZ, 1, E), F32),
         V((NX * NC, ITM, E), F32),
-        V((NX, ITM, E), F32),
-        V((2, ITM // 2, E), F32),
-        V((2, ITM, E), F32),
-        D((128,)),
+        V((NX, ITM, E), I16), V((NX, 1, E), F32),
+        V((NX, ITM, E), I16), V((NX, 1, E), F32),
+        V((2, HE, E), I16), V((2, 1, E), F32),
+        V((4, HE, E), I16), V((4, 1, E), F32),
+        V((2, HE, E), I16), V((2, 1, E), F32),
+        V((4, HE, E), I16), V((4, 1, E), F32),
+        D((3,)),
+        D((144,)),
         D((NY * NZ,)),
         D((2 * NX * NC,)),
         D((NY,)), D((NY,)), D((NZ,)), D((NZ,)),
-        D((2,)), D((4,)), D((NZ,)), D((NX,)), D((2,)), D((4,)),
+        D((2, 2)), D((4, 2)), D((NZ, 2)), D((NX, 2)), D((2, 2)), D((4, 2)),
     ]
+    outs = (
+        jax.ShapeDtypeStruct((1, 128), F32),
+        jax.ShapeDtypeStruct((OWN, E), F32),
+        jax.ShapeDtypeStruct((ITM, E), F32),
+    )
+    hbm = pl.BlockSpec(memory_space=pl.ANY)
     loss, ug, ig = pl.pallas_call(
         kernel,
-        out_shape=(
-            jax.ShapeDtypeStruct((1, 128), F32),
-            jax.ShapeDtypeStruct((OWN, E), F32),
-            jax.ShapeDtypeStruct((ITM, E), F32),
-        ),
-        in_specs=[pl.BlockSpec(memory_space=pltpu.VMEM)] * 2,
+        out_shape=outs,
+        in_specs=[hbm] * 3,
         out_specs=tuple([pl.BlockSpec(memory_space=pltpu.VMEM)] * 3),
         scratch_shapes=scratch,
         compiler_params=pltpu.CompilerParams(
             collective_id=0, has_side_effects=True, vmem_limit_bytes=60 * 2**20
         ),
         name="infonce",
-    )(blk, items)
+    )(users, items, pos_ids.reshape(1, OWN))
+    loss, ug, ig = pl.pallas_call(
+        finish,
+        out_shape=outs,
+        in_specs=[hbm] * 3,
+        out_specs=tuple([hbm] * 3),
+        scratch_shapes=[V(o.shape, o.dtype) for o in outs] + [D((6,))],
+        name="finish",
+    )(loss, ug, ig)
     return loss[0, :OWN], ug, ig
 
 

time: 71 us -> 65.4 us (0.921)
  the two profiles are of different devices: /device:TPU:1 before, /device:TPU:2 now
where the time goes in v2:
time: 65.4 us; the launch traced here: 65.3 us
  Pallas kernels  63.4 us (97%)
  local copies, waits for them, and re-layouts  1.16 us (2%)
    pallas_call x1, Pallas kernels, local(): pl.pallas_call(kernel, out_shape=outs, in_specs=[hbm] * 3, out_specs=tupl...  61.7 us
    pallas_call x1, Pallas kernels, local(): pl.pallas_call(finish, out_shape=outs, in_specs=[hbm] * 3, out_specs=tupl...  1.71 us

profile of v2, /device:TPU:2, one launch (start us, length us, event | category | flops | bytes accessed | tf_op | source)
XLA Modules:
  0.0 65.3 jit_solution(15208135119705153256)
XLA Ops:
  0.6 61.7 %infonce.1 = (f32[1,128]{1,0:T(1,128)}, f32[40,256]{1,0:T(8,128)}, f32[256,256]{1,0:T(8,128)}) custom-call(bf16[40,256]{1,0:T(8,128)(2,1)} %users.1, bf16[256,256]{1,0:T(8,128)(2,1)} %items.1, s32[1,40]{1,0:T(1,128)} %bitcast.3), custom_call_target="tpu_custom_call" | custom-call | tf_op jit(solution)/shard_map/infonce/pallas_call | solution.py:466
  62.4 1.7 %finish.1 = (f32[1,128]{1,0:T(1,128)}, f32[40,256]{1,0:T(8,128)}, f32[256,256]{1,0:T(8,128)}) custom-call(f32[1,128]{1,0:T(1,128)} %get-tuple-element.9.loss, f32[40,256]{1,0:T(8,128)} %get-tuple-element.10.ug, f32[256,256]{1,0:T(8,128)} %get-tuple-element.11.ig), custom_call_target="tpu_custom_call" | custom-call | tf_op jit(solution)/shard_map/finish/pallas_call | solution.py:477
  64.1 0.0 copy-start
  64.1 0.6 copy-done
  64.8 0.5 slice_bitcast_fusion
Async XLA Ops:
  64.1 0.7 %copy-start = (f32[1,128]{1,0:T(1,128)S(1)}, f32[1,128]{1,0:T(1,128)}, u32[]{:S(2)}) copy-start(f32[1,128]{1,0:T(1,128)} %get-tuple-element.12) | copy-start | bytes 1540

commit v3 on v2

--- a/solution.py
+++ b/solution.py
@@ -34,9 +34,9 @@
     return q.astype(F32) * (m * (1.0 / TOP))
 
 
-def kernel(users, items, ids, loss_out, ug_out, ig_out, U, I, ID, IT, UT, HL, LG, EX, MB, SB, PB, W, ST, PT, YST, YPT, ZST, ZPT,
+def kernel(users, items, ids, loss_out, ug_out, ig_out, U, I, ID, IT, UT, HL, LGA, LGB, EX, MB, SB, PB, W, ST, PT, YST, YPT, ZST, ZPT,
            SC, UG, UZ, QY2, MY2, QY1, MY1, YQ2, YM2, YQ1, YM1, QZ, MZ, ZQ, ZM, G, QP, MP, PQ, PM, QX2, MX2, QX1, MX1, XQ2, XM2,
-           XQ1, XM1, s_in, s_send, s_u, s_i, s_ys, s_yp, s_zs, s_zp, s_y2, s_y1, s_zr, s_pg, s_x2, s_x1):
+           XQ1, XM1, OL, OU, OI, s_in, s_out, s_send, s_u, s_i, s_ys, s_yp, s_zs, s_zp, s_y2, s_y1, s_zr, s_pg, s_x2, s_x1):
     xh, z, xl, y, c = (lax.axis_index(a) for a in AXES)
     x = 2 * xh + xl
 
@@ -49,11 +49,18 @@
 
     def send(src, dst, recv, where):
         copy = pltpu.make_async_remote_copy(
-            src_ref=src, dst_ref=dst, send_sem=s_send.at[len(sent)], recv_sem=recv,
+            src_ref=src, dst_ref=dst, send_sem=s_send.at[0], recv_sem=recv,
             device_id=where, device_id_type=MESH,
         )
         copy.start()
         sent.append(copy)
+
+    stored = []
+
+    def store(src, dst, i):
+        copy = pltpu.make_async_copy(src, dst, s_out.at[i])
+        copy.start()
+        stored.append(copy)
 
     def arrived(dst, recv):
         pltpu.make_async_remote_copy(
@@ -67,7 +74,7 @@
     co = 1 - c
 
     mine = y * NZ + z
-    bo = x * NC + c
+    bo = c * NX + x
     inputs = [
         pltpu.make_async_copy(users, U.at[mine, pl.ds(0, OWN)], s_in.at[0]),
         pltpu.make_async_copy(items, I.at[bo], s_in.at[1]),
@@ -114,7 +121,7 @@
             send(U.at[s], U.at[s], s_u.at[s], dev(dy=dy))
 
     for dx, keep in ((3, 0), (1, 1)):
-        b = xx[dx] * NC + c
+        b = c * NX + xx[dx]
         for h, ref, sem in halves(b, (keep, 1 - keep)):
             arrived(ref, sem)
             if h == keep:
@@ -145,27 +152,45 @@
 
     rows = lax.broadcasted_iota(jnp.int32, (ITM, 128), 0).astype(F32)
 
-    def first(yi, bx, bc):
-        b = bx * NC + bc
-        LG[...] = jnp.dot(I[b], UT[yi], preferred_element_type=F32)
-        at = target(yi, bx, bc)
+    def logits(yi, b, lg):
+        lg[...] = jnp.dot(I[b], UT[yi], preferred_element_type=F32)
+
+    def exponents(yi, b, lg):
+        at = target(yi, lax.rem(b, NX), b // NX)
         for j in range(CH // 128):
             cols = slice(128 * j, 128 * j + 128)
-            lg = LG[:, cols]
-            top = jnp.max(lg, axis=0, keepdims=True)
-            ex = jnp.exp(lg - top)
+            part = lg[:, cols]
+            top = jnp.max(part, axis=0, keepdims=True)
+            ex = jnp.exp(part - top)
             EX[b, yi, :, cols] = ex
             MB[yi, b, :, cols] = top
             SB[yi, b, :, cols] = jnp.sum(ex, axis=0, keepdims=True)
-            PB[yi, b, :, cols] = jnp.sum(jnp.where(rows == at[:, cols], lg, 0.0), axis=0, keepdims=True)
+            PB[yi, b, :, cols] = jnp.sum(jnp.where(rows == at[:, cols], part, 0.0), axis=0, keepdims=True)
+
+    def first(yi, b):
+        logits(yi, b, LGA)
+        exponents(yi, b, LGA)
+
+    def first_all(yi):
+        logits(yi, 0, LGA)
+
+        def two(i, _):
+            logits(yi, 2 * i + 1, LGB)
+            exponents(yi, 2 * i, LGA)
+            logits(yi, lax.rem(2 * i + 2, NX * NC), LGA)
+            exponents(yi, 2 * i + 1, LGB)
+            return 0
+
+        lax.fori_loop(0, NX * NC // 2, two, 0)
 
     def turn(b):
-        IT[b] = I[b].T
+        IT[:, pl.ds(pl.multiple_of(b * ITM, ITM), ITM)] = I[b].T
 
     place_ids(yy[0])
     for dx in (0, 3, 1):
-        first(yy[0], xx[dx], c)
-        turn(xx[dx] * NC + c)
+        b = c * NX + xx[dx]
+        first(yy[0], b)
+        turn(b)
 
     for dy, first_z in ((3, 0), (1, 1)):
         for d in range(NZ):
@@ -174,94 +199,96 @@
             if (d < NZ // 2) == (first_z == 0):
                 send(U.at[s], U.at[s], s_u.at[s], dev(dy=4 - dy))
 
-    b = xx[2] * NC + c
+    b = c * NX + xx[2]
     for h, ref, sem in halves(b):
         arrived(ref, sem)
         send(ref, ref, sem, dev(dc=1))
-    first(yy[0], xx[2], c)
+    first(yy[0], b)
     turn(b)
     for dx in (0, 3, 1, 2):
-        b = xx[dx] * NC + co
+        b = co * NX + xx[dx]
         for h, ref, sem in halves(b):
             arrived(ref, sem)
-        first(yy[0], xx[dx], co)
+        first(yy[0], b)
         turn(b)
 
     for dy in (3, 1):
         place_ids(yy[dy])
-        lax.fori_loop(0, NX * NC, lambda i, _: (first(yy[dy], i // NC, lax.rem(i, NC)), 0)[1], 0)
+        first_all(yy[dy])
     for d in range(NZ):
         s = yy[2] * NZ + d
         arrived(U.at[s], s_u.at[s])
     place_ids(yy[2])
-    lax.fori_loop(0, NX * NC, lambda i, _: (first(yy[2], i // NC, lax.rem(i, NC)), 0)[1], 0)
+    first_all(yy[2])
 
     NR = CH // 128
     for k in range(NY):
         m = jnp.max(MB[k], axis=0)
         s = jnp.sum(SB[k] * jnp.exp(MB[k] - m[None]), axis=0)
+        line = m + jnp.log(s)
         p = jnp.sum(PB[k], axis=0)
         for j in range(NR):
             cols = slice(128 * j, 128 * j + 128)
-            r = NR * k + j
-            ST[r : r + 1] = m[:, cols]
-            ST[12 + r : 13 + r] = s[:, cols]
-            PT[r : r + 1] = p[:, cols]
-    PT[12:16] = jnp.zeros((4, 128), F32)
+            ST[NR * k + j : NR * k + j + 1] = line[:, cols]
+            PT[k, j : j + 1] = p[:, cols]
+        PT[k, NR:8] = jnp.zeros((8 - NR, 128), F32)
+    ST[12:16] = jnp.zeros((4, 128), F32)
 
     def combine(parts):
-        m = parts[0][0:12]
+        m = parts[0]
         for q in parts[1:]:
-            m = jnp.maximum(m, q[0:12])
+            m = jnp.maximum(m, q)
         s = jnp.zeros_like(m)
         for q in parts:
-            s = s + q[12:24] * jnp.exp(q[0:12] - m)
-        return m, s
-
-    for d in (1, 3, 2):
+            s = s + jnp.exp(q - m)
+        return m + jnp.log(s)
+
+    for d in (2, 1, 3):
         send(ST, YST.at[y], s_ys.at[y], dev(dy=d))
-    for d in (1, 3, 2):
-        send(PT, YPT.at[y], s_yp.at[y], dev(dy=d))
+    for d in (2, 1, 3):
+        send(PT.at[yy[d]], YPT.at[y], s_yp.at[y], dev(dy=d))
     for d in (1, 3, 2):
         arrived(YST.at[yy[d]], s_ys.at[yy[d]])
     YST[y] = ST[...]
-    m, s = combine([YST[k] for k in range(NY)])
-    ZST[z, 0:12] = m
-    ZST[z, 12:24] = s
+    ZST[z] = combine([YST[k] for k in range(NY)])
     for d in (4, 3, 5, 2, 6, 1, 7):
         send(ZST.at[z], ZST.at[z], s_zs.at[z], dev(dz=d))
     for d in (1, 3, 2):
         arrived(YPT.at[yy[d]], s_yp.at[yy[d]])
-    YPT[y] = PT[...]
-    ZPT[z] = (YPT[0] + YPT[1]) + (YPT[2] + YPT[3])
+    ZPT[z] = PT[y] + YPT[yy[1]] + YPT[yy[2]] + YPT[yy[3]]
     for d in (4, 3, 5, 2, 6, 1, 7):
         send(ZPT.at[z], ZPT.at[z], s_zp.at[z], dev(dz=d))
     for d in (1, 7, 2, 6, 3, 5, 4):
         arrived(ZST.at[zz[d]], s_zs.at[zz[d]])
-    m, s = combine([ZST[k] for k in range(NZ)])
-    lse = m + jnp.log(s)
+    lse = combine([ZST[k] for k in range(NZ)])
     for k in range(NY):
         for j in range(NR):
             r = NR * k + j
             SC[k, :, 128 * j : 128 * j + 128] = lse[r : r + 1]
 
-    def second(yi, bx, bc):
-        b = bx * NC + bc
+    def span(yi):
+        return pl.ds(pl.multiple_of(yi * CH, CH), CH)
+
+    def second(yi, b):
+        bx, bc = lax.rem(b, NX), b // NX
         at = target(yi, bx, bc)
         scale = jnp.where(valid, jnp.exp(MB[yi, b] - SC[yi]), 0.0)
         for j in range(CH // 128):
             cols = slice(128 * j, 128 * j + 128)
             w = EX[b, yi, :, cols] * scale[:, cols]
             w = w - jnp.where(rows == at[:, cols], 1.0, 0.0)
-            W[b, yi, :, cols] = w.astype(BF16)
+            W[bc, bx, :, pl.ds(pl.multiple_of(yi * CH + 128 * j, 128), 128)] = w.astype(BF16)
+
+    def weights(yi):
+        lax.fori_loop(0, NX * NC, lambda b, _: (second(yi, b), 0)[1], 0)
+
+    def user_dot(d):
+        w = W[:, :, :, span(yy[d])].reshape(NC * NX * ITM, CH)
+        UG[d] = jnp.dot(IT[...], w, preferred_element_type=F32)
 
     def user_terms(d):
-        yi = yy[d]
-        lax.fori_loop(0, NX * NC, lambda i, _: (second(yi, i // NC, lax.rem(i, NC)), 0)[1], 0)
-        acc = jnp.dot(IT[0], W[0, yi], preferred_element_type=F32)
-        for b in range(1, NX * NC):
-            acc += jnp.dot(IT[b], W[b, yi], preferred_element_type=F32)
-        UG[d] = acc
+        weights(yy[d])
+        user_dot(d)
 
     H = E // 2
     half = [pl.ds(0, H), pl.ds(H, H)]
@@ -296,22 +323,52 @@
     direct(1, 0)
     user_terms(3)
     direct(3, 1)
+    weights(yy[0])
     relayed(1, 0)
     relayed(3, 1)
-    user_terms(0)
-
-    def item_terms(b):
-        acc = jnp.dot(W[b, 0], U[0:NZ].reshape(CH, E), preferred_element_type=F32)
-        for k in range(1, NY):
-            acc += jnp.dot(W[b, k], U[k * NZ : k * NZ + NZ].reshape(CH, E), preferred_element_type=F32)
-        G[b] = acc
+
+    everyone = NY * NZ * ROW
+
+    def item_terms(bc, bx):
+        w = W[bc, bx]
+        G[bc * NX + bx] = jnp.dot(w, U[...].reshape(everyone, E), preferred_element_type=F32)
 
     for dx in (2, 1, 3, 0):
-        b = xx[dx] * NC + co
-        item_terms(b)
+        item_terms(co, xx[dx])
+        b = co * NX + xx[dx]
         code(G[b], QP.at[dx], MP.at[dx])
         send2(QP.at[dx], PQ.at[dx], MP.at[dx], PM.at[dx], s_pg, dx, dev(dc=1))
-
+    user_dot(0)
+
+    def own_terms(dx):
+        b = c * NX + xx[dx]
+        item_terms(c, xx[dx])
+        arrived2(PQ.at[dx], PM.at[dx], s_pg, dx)
+        G[b] += decode(PQ[dx], PM[dx])
+        return b
+
+    b2 = own_terms(2)
+    for i in range(2):
+        code(G[b2, H * i : H * i + H], QX2.at[i], MX2.at[i])
+        send2(QX2.at[i], XQ2.at[i], MX2.at[i], XM2.at[i], s_x2, i, dev(dx=1 + 2 * i))
+
+    def x_direct(dx, i):
+        b = own_terms(dx)
+        h = 1 - i
+        k = 2 * i + h
+        code(G[b, H * h : H * h + H], QX1.at[k], MX1.at[k])
+        send2(QX1.at[k], XQ1.at[k], MX1.at[k], XM1.at[k], s_x1, k, dev(dx=dx))
+        return b
+
+    def x_relayed(b, dx, i):
+        h = i
+        k = 2 * i + h
+        arrived2(XQ2.at[i], XM2.at[i], s_x2, i)
+        code(G[b, H * h : H * h + H] + decode(XQ2[i], XM2[i]), QX1.at[k], MX1.at[k])
+        send2(QX1.at[k], XQ1.at[k], MX1.at[k], XM1.at[k], s_x1, k, dev(dx=dx))
+
+    b1 = x_direct(1, 0)
+    b3 = x_direct(3, 1)
     total = []
     for h in range(2):
         v = UG[0, H * h : H * h + H]
@@ -325,35 +382,6 @@
         code(UZ[zz[d], 0:OWN], QZ.at[d], MZ.at[d])
         send2(QZ.at[d], ZQ.at[d], MZ.at[d], ZM.at[d], s_zr, d, dev(dz=d))
 
-    def own_terms(dx):
-        b = xx[dx] * NC + c
-        item_terms(b)
-        arrived2(PQ.at[dx], PM.at[dx], s_pg, dx)
-        G[b] += decode(PQ[dx], PM[dx])
-        return b
-
-    b2 = own_terms(2)
-    for i in range(2):
-        code(G[b2, H * i : H * i + H], QX2.at[i], MX2.at[i])
-        send2(QX2.at[i], XQ2.at[i], MX2.at[i], XM2.at[i], s_x2, i, dev(dx=1 + 2 * i))
-
-    def x_direct(dx, i):
-        b = own_terms(dx)
-        h = 1 - i
-        k = 2 * i + h
-        code(G[b, H * h : H * h + H], QX1.at[k], MX1.at[k])
-        send2(QX1.at[k], XQ1.at[k], MX1.at[k], XM1.at[k], s_x1, k, dev(dx=dx))
-        return b
-
-    def x_relayed(b, dx, i):
-        h = i
-        k = 2 * i + h
-        arrived2(XQ2.at[i], XM2.at[i], s_x2, i)
-        code(G[b, H * h : H * h + H] + decode(XQ2[i], XM2[i]), QX1.at[k], MX1.at[k])
-        send2(QX1.at[k], XQ1.at[k], MX1.at[k], XM1.at[k], s_x1, k, dev(dx=dx))
-
-    b1 = x_direct(1, 0)
-    b3 = x_direct(3, 1)
     x_relayed(b1, 1, 0)
     x_relayed(b3, 3, 1)
     b0 = own_terms(0)
@@ -363,22 +391,22 @@
     pos = ZPT[0]
     for k in range(1, NZ):
         pos = pos + ZPT[k]
-    for k in range(NY):
-        for j in range(NR):
-            r = NR * k + j
-            PB[k, 0, :, 128 * j : 128 * j + 128] = lse[r : r + 1] - pos[r : r + 1]
-    line = PB[y, 0]
+    for j in range(NR):
+        PB[0, 0, :, 128 * j : 128 * j + 128] = pos[j : j + 1]
+    line = SC[y] - PB[0, 0]
     out = line[:, 0:ROW]
     for k in range(1, NZ):
         out = jnp.where(z == k, line[:, ROW * k : ROW * k + ROW], out)
-    loss_out[:, 0:ROW] = out
-    loss_out[:, ROW:128] = jnp.zeros((1, 128 - ROW), F32)
+    OL[:, 0:ROW] = out
+    OL[:, ROW:128] = jnp.zeros((1, 128 - ROW), F32)
+    loss_out[...] = OL[...]
 
     total = UZ[z, 0:OWN]
     for d in (1, 7, 2, 6, 3, 5, 4):
         arrived2(ZQ.at[d], ZM.at[d], s_zr, d)
         total = total + decode(ZQ[d], ZM[d])
-    ug_out[...] = total
+    OU[...] = total
+    ug_out[...] = OU[...]
 
     for h in range(2):
         v = G[b0, H * h : H * h + H]
@@ -386,28 +414,23 @@
             k = 2 * i + h
             arrived2(XQ1.at[k], XM1.at[k], s_x1, k)
             v = v + decode(XQ1[k], XM1[k])
-        ig_out[H * h : H * h + H] = v
+        OI[H * h : H * h + H] = v
+        ig_out[H * h : H * h + H] = OI[H * h : H * h + H]
 
     for copy in sent:
         copy.wait_send()
-
-
-def finish(loss, ug, ig, loss_out, ug_out, ig_out, vl, vu, vi, sem):
-    into = [
-        pltpu.make_async_copy(a, b, sem.at[k])
-        for k, (a, b) in enumerate(((ig, vi), (ug, vu), (loss, vl)))
-    ]
-    out = [
-        pltpu.make_async_copy(a, b, sem.at[k + 3])
-        for k, (a, b) in enumerate(((vi, ig_out), (vu, ug_out), (vl, loss_out)))
-    ]
-    for copy in into:
+    for copy in stored:
+        copy.wait()
+
+
+def finish(loss, ug, ig, loss_out, ug_out, ig_out, vl, sem):
+    out = [pltpu.make_async_copy(a, b, sem.at[k]) for k, (a, b) in enumerate(((ig, ig_out), (ug, ug_out)))]
+    for copy in out:
         copy.start()
-    for a, b in zip(into, out):
-        a.wait()
-        b.start()
     for copy in out:
         copy.wait()
+    pltpu.sync_copy(loss, vl)
+    loss_out[...] = vl[0, 0:OWN]
 
 
 def local(users, items, pos_ids):
@@ -419,21 +442,22 @@
         V((NY * NZ, ROW, E), BF16),
         V((NX * NC, ITM, E), BF16),
         V((1, OWN), jnp.int32),
-        V((NX * NC, E, ITM), BF16),
+        V((E, NX * NC * ITM), BF16),
         V((NY, E, CH), BF16),
         V((NY, 2, 1, CH), F32),
+        V((ITM, CH), F32),
         V((ITM, CH), F32),
         V((NX * NC, NY, ITM, CH), F32),
         V((NY, NX * NC, 1, CH), F32),
         V((NY, NX * NC, 1, CH), F32),
         V((NY, NX * NC, 1, CH), F32),
-        V((NX * NC, NY, ITM, CH), BF16),
-        V((24, 128), F32),
+        V((NC, NX, ITM, NY * CH), BF16),
         V((16, 128), F32),
-        V((NY, 24, 128), F32),
+        V((NY, 8, 128), F32),
         V((NY, 16, 128), F32),
-        V((NZ, 24, 128), F32),
+        V((NY, 8, 128), F32),
         V((NZ, 16, 128), F32),
+        V((NZ, 8, 128), F32),
         V((NY, 1, CH), F32),
         V((NY, E, CH), F32),
         V((NZ, ROW, E), F32),
@@ -450,8 +474,10 @@
         V((4, HE, E), I16), V((4, 1, E), F32),
         V((2, HE, E), I16), V((2, 1, E), F32),
         V((4, HE, E), I16), V((4, 1, E), F32),
+        V((1, 128), F32), V((OWN, E), F32), V((ITM, E), F32),
         D((3,)),
-        D((144,)),
+        D((4,)),
+        D((1,)),
         D((NY * NZ,)),
         D((2 * NX * NC,)),
         D((NY,)), D((NY,)), D((NZ,)), D((NZ,)),
@@ -462,27 +488,27 @@
         jax.ShapeDtypeStruct((OWN, E), F32),
         jax.ShapeDtypeStruct((ITM, E), F32),
     )
-    hbm = pl.BlockSpec(memory_space=pl.ANY)
+    hbm = pl.BlockSpec(memory_space=pltpu.HBM)
     loss, ug, ig = pl.pallas_call(
         kernel,
-        out_shape=outs,
+        out_shape=tuple(pltpu.VMEM(o.shape, o.dtype) for o in outs),
         in_specs=[hbm] * 3,
         out_specs=tuple([pl.BlockSpec(memory_space=pltpu.VMEM)] * 3),
         scratch_shapes=scratch,
         compiler_params=pltpu.CompilerParams(
-            collective_id=0, has_side_effects=True, vmem_limit_bytes=60 * 2**20
+            collective_id=0, has_side_effects=True, vmem_limit_bytes=40 * 2**20
         ),
         name="infonce",
-    )(users, items, pos_ids.reshape(1, OWN))
-    loss, ug, ig = pl.pallas_call(
+    )(*(pltpu.with_memory_space_constraint(a, pltpu.HBM) for a in (users, items, pos_ids.reshape(1, OWN))))
+    return pl.pallas_call(
         finish,
-        out_shape=outs,
-        in_specs=[hbm] * 3,
-        out_specs=tuple([hbm] * 3),
-        scratch_shapes=[V(o.shape, o.dtype) for o in outs] + [D((6,))],
+        out_shape=(jax.ShapeDtypeStruct((OWN,), F32), *outs[1:]),
+        in_specs=[pl.BlockSpec(memory_space=pl.ANY)] * 3,
+        out_specs=(pl.BlockSpec(memory_space=pltpu.VMEM), hbm, hbm),
+        scratch_shapes=[V((1, 128), F32), D((2,))],
+        compiler_params=pltpu.CompilerParams(vmem_limit_bytes=2**20),
         name="finish",
     )(loss, ug, ig)
-    return loss[0, :OWN], ug, ig
 
 
 def solution(mesh):

time: 65.4 us -> 57.7 us (0.88)
  Pallas kernels: 63.4 us -> 57 us
  local copies, waits for them, and re-layouts: 1.16 us -> 0 us
    pallas_call x2, Pallas kernels: 63.4 us -> 57 us  [the longest x1 55.7 us: local(): pl.pallas_call(kernel, out_shape=tuple((pltpu.VMEM(o.shape, o.dtype) for...]
where the time goes in v3:
time: 57.7 us; the launch traced here: 57.6 us
  Pallas kernels  57 us (99%)
  between operations  0.64 us (1%)
    pallas_call x1, Pallas kernels, local(): pl.pallas_call(kernel, out_shape=tuple((pltpu.VMEM(o.shape, o.dtype) for...  55.7 us
    pallas_call x1, Pallas kernels, local(): pl.pallas_call(finish, out_shape=(jax.ShapeDtypeStruct((OWN,), F32), *out...  1.24 us

profile of v3, /device:TPU:2, one launch (start us, length us, event | category | flops | bytes accessed | tf_op | source)
XLA Modules:
  0.0 57.6 jit_solution(15583372875343864207)
XLA Ops:
  0.6 55.7 %infonce.1 = (f32[1,128]{1,0:T(1,128)S(1)}, f32[40,256]{1,0:T(8,128)S(1)}, f32[256,256]{1,0:T(8,128)S(1)}) custom-call(bf16[40,256]{1,0:T(8,128)(2,1)} %users.1, bf16[256,256]{1,0:T(8,128)(2,1)} %items.1, s32[1,40]{1,0:T(1,128)} %bitcast.1), custom_call_target="tpu_custom_call" | custom-call | tf_op jit(solution)/shard_map/infonce/pallas_call | solution.py:492
  56.3 1.2 %finish.1 = (f32[40]{0:T(128)}, f32[40,256]{1,0:T(8,128)}, f32[256,256]{1,0:T(8,128)}) custom-call(f32[1,128]{1,0:T(1,128)S(1)} %get-tuple-element.6.loss, f32[40,256]{1,0:T(8,128)S(1)} %get-tuple-element.7.ug, f32[256,256]{1,0:T(8,128)S(1)} %get-tuple-element.8.ig), custom_call_target="tpu_custom_call" | custom-call | tf_op jit(solution)/shard_map/finish/pallas_call | solution.py:503

commit v4 on v3

--- a/solution.py
+++ b/solution.py
@@ -114,20 +114,6 @@
     for h, dst, sem in halves(bo):
         send(dst, dst, sem, dev(dc=1))
 
-    for d in (1, 7, 2, 6, 3, 5, 4):
-        s = y * NZ + zz[d]
-        arrived(U.at[s], s_u.at[s])
-        for dy in (1, 3):
-            send(U.at[s], U.at[s], s_u.at[s], dev(dy=dy))
-
-    for dx, keep in ((3, 0), (1, 1)):
-        b = c * NX + xx[dx]
-        for h, ref, sem in halves(b, (keep, 1 - keep)):
-            arrived(ref, sem)
-            if h == keep:
-                send(ref, ref, sem, dev(dx=4 - dx))
-            send(ref, ref, sem, dev(dc=1))
-
     def place_ids(yi):
         UT[yi] = U[pl.ds(yi * NZ, NZ)].reshape(CH, E).T
         part = U[pl.ds(yi * NZ, NZ), OWN:ROW, 0:128].astype(F32)
@@ -146,71 +132,108 @@
     valid = n1 - ((n1 * 1366) >> 16) * ROW < OWN
 
     def target(yi, bx, bc):
-        owner = (bx // 2) * 128 + z * 16 + lax.rem(bx, 2) * 8 + y * 2 + bc
+        owner = (bx // 2) * 128 + z * 16 + (bx % 2) * 8 + y * 2 + bc
         match = (HL[yi, 0] == owner.astype(F32)) & valid
         return jnp.where(match, HL[yi, 1], -1.0)
 
     rows = lax.broadcasted_iota(jnp.int32, (ITM, 128), 0).astype(F32)
 
-    def logits(yi, b, lg):
-        lg[...] = jnp.dot(I[b], UT[yi], preferred_element_type=F32)
-
-    def exponents(yi, b, lg):
+    def logits(yi, b, n, lg):
+        lg[0 : n * ITM] = jnp.dot(I[pl.ds(b, n)].reshape(n * ITM, E), UT[yi], preferred_element_type=F32)
+
+    def exponents(yi, b, h, lg):
         at = target(yi, lax.rem(b, NX), b // NX)
         for j in range(CH // 128):
             cols = slice(128 * j, 128 * j + 128)
-            part = lg[:, cols]
+            part = lg[h * ITM : h * ITM + ITM, cols]
             top = jnp.max(part, axis=0, keepdims=True)
             ex = jnp.exp(part - top)
             EX[b, yi, :, cols] = ex
             MB[yi, b, :, cols] = top
             SB[yi, b, :, cols] = jnp.sum(ex, axis=0, keepdims=True)
-            PB[yi, b, :, cols] = jnp.sum(jnp.where(rows == at[:, cols], part, 0.0), axis=0, keepdims=True)
-
-    def first(yi, b):
-        logits(yi, b, LGA)
-        exponents(yi, b, LGA)
+            hit = jnp.zeros((8, 128), F32)
+            for r in range(0, ITM, 8):
+                hit = jnp.where(rows[r : r + 8] == at[:, cols], part[r : r + 8], hit)
+            PB[yi, b, :, cols] = jnp.sum(hit, axis=0, keepdims=True)
+
+    def first_some(yi, blocks):
+        held = (LGA, LGB)
+        logits(yi, blocks[0], 1, LGA)
+        for k, b in enumerate(blocks):
+            if k + 1 < len(blocks):
+                logits(yi, blocks[k + 1], 1, held[(k + 1) % 2])
+            exponents(yi, b, 0, held[k % 2])
 
     def first_all(yi):
-        logits(yi, 0, LGA)
-
-        def two(i, _):
-            logits(yi, 2 * i + 1, LGB)
-            exponents(yi, 2 * i, LGA)
-            logits(yi, lax.rem(2 * i + 2, NX * NC), LGA)
-            exponents(yi, 2 * i + 1, LGB)
+        logits(yi, 0, 2, LGA)
+
+        def four(i, _):
+            logits(yi, 4 * i + 2, 2, LGB)
+            exponents(yi, 4 * i, 0, LGA)
+            exponents(yi, 4 * i + 1, 1, LGA)
+            logits(yi, lax.rem(4 * i + 4, NX * NC), 2, LGA)
+            exponents(yi, 4 * i + 2, 0, LGB)
+            exponents(yi, 4 * i + 3, 1, LGB)
             return 0
 
-        lax.fori_loop(0, NX * NC // 2, two, 0)
+        lax.fori_loop(0, NX * NC // 4, four, 0)
 
     def turn(b):
         IT[:, pl.ds(pl.multiple_of(b * ITM, ITM), ITM)] = I[b].T
 
-    place_ids(yy[0])
-    for dx in (0, 3, 1):
-        b = c * NX + xx[dx]
-        first(yy[0], b)
-        turn(b)
-
-    for dy, first_z in ((3, 0), (1, 1)):
-        for d in range(NZ):
-            s = yy[dy] * NZ + d
+    UP = (0, 7, 2, 5)
+
+    def from_z(d):
+        s = y * NZ + zz[d]
+        arrived(U.at[s], s_u.at[s])
+        for dy in (1, 3):
+            send(U.at[s], U.at[s], s_u.at[s], dev(dy=dy))
+
+    def from_y(d):
+        for dy in (3, 1):
+            s = yy[dy] * NZ + zz[d]
             arrived(U.at[s], s_u.at[s])
-            if (d < NZ // 2) == (first_z == 0):
+            if (d in UP) == (dy == 3):
                 send(U.at[s], U.at[s], s_u.at[s], dev(dy=4 - dy))
 
-    b = c * NX + xx[2]
-    for h, ref, sem in halves(b):
-        arrived(ref, sem)
-        send(ref, ref, sem, dev(dc=1))
-    first(yy[0], b)
-    turn(b)
-    for dx in (0, 3, 1, 2):
+    def from_x(step):
+        for dx, keep in ((3, 0), (1, 1)):
+            b = c * NX + xx[dx]
+            h, ref, sem = halves(b, (keep, 1 - keep))[step]
+            arrived(ref, sem)
+            if step == 0:
+                send(ref, ref, sem, dev(dx=4 - dx))
+            send(ref, ref, sem, dev(dc=1))
+
+    def from_x2():
+        for h, ref, sem in halves(c * NX + xx[2]):
+            arrived(ref, sem)
+            send(ref, ref, sem, dev(dc=1))
+
+    def from_partner(dx):
         b = co * NX + xx[dx]
         for h, ref, sem in halves(b):
             arrived(ref, sem)
-        first(yy[0], b)
-        turn(b)
+        return b
+
+    for d in (1, 7, 2, 6):
+        from_z(d)
+    from_y(0)
+    from_x(0)
+    for d in (3, 5, 4):
+        from_z(d)
+    from_x(1)
+    place_ids(yy[0])
+    first_some(yy[0], [c * NX + xx[dx] for dx in (0, 3, 1)])
+    from_y(1)
+    from_y(7)
+    from_x2()
+    from_y(2)
+    from_y(6)
+    first_some(yy[0], [from_partner(dx) for dx in (0, 3, 1)])
+    for d in (3, 5, 4):
+        from_y(d)
+    first_some(yy[0], [c * NX + xx[2], from_partner(2)])
 
     for dy in (3, 1):
         place_ids(yy[dy])
@@ -244,22 +267,20 @@
         return m + jnp.log(s)
 
     for d in (2, 1, 3):
-        send(ST, YST.at[y], s_ys.at[y], dev(dy=d))
+        send(ST, YST.at[y], s_ys.at[0], dev(dy=d))
     for d in (2, 1, 3):
-        send(PT.at[yy[d]], YPT.at[y], s_yp.at[y], dev(dy=d))
-    for d in (1, 3, 2):
-        arrived(YST.at[yy[d]], s_ys.at[yy[d]])
+        send(PT.at[yy[d]], YPT.at[y], s_yp.at[0], dev(dy=d))
+    lax.fori_loop(0, NX * NC, lambda b, _: (turn(b), 0)[1], 0)
+    arrived(YST.at[pl.ds(0, NY - 1)], s_ys.at[0])
     YST[y] = ST[...]
     ZST[z] = combine([YST[k] for k in range(NY)])
     for d in (4, 3, 5, 2, 6, 1, 7):
-        send(ZST.at[z], ZST.at[z], s_zs.at[z], dev(dz=d))
-    for d in (1, 3, 2):
-        arrived(YPT.at[yy[d]], s_yp.at[yy[d]])
+        send(ZST.at[z], ZST.at[z], s_zs.at[0], dev(dz=d))
+    arrived(YPT.at[pl.ds(0, NY - 1)], s_yp.at[0])
     ZPT[z] = PT[y] + YPT[yy[1]] + YPT[yy[2]] + YPT[yy[3]]
     for d in (4, 3, 5, 2, 6, 1, 7):
-        send(ZPT.at[z], ZPT.at[z], s_zp.at[z], dev(dz=d))
-    for d in (1, 7, 2, 6, 3, 5, 4):
-        arrived(ZST.at[zz[d]], s_zs.at[zz[d]])
+        send(ZPT.at[z], ZPT.at[z], s_zp.at[0], dev(dz=d))
+    arrived(ZST.at[pl.ds(0, NZ - 1)], s_zs.at[0])
     lse = combine([ZST[k] for k in range(NZ)])
     for k in range(NY):
         for j in range(NR):
@@ -270,7 +291,7 @@
         return pl.ds(pl.multiple_of(yi * CH, CH), CH)
 
     def second(yi, b):
-        bx, bc = lax.rem(b, NX), b // NX
+        bx, bc = b % NX, b // NX
         at = target(yi, bx, bc)
         scale = jnp.where(valid, jnp.exp(MB[yi, b] - SC[yi]), 0.0)
         for j in range(CH // 128):
@@ -280,7 +301,8 @@
             W[bc, bx, :, pl.ds(pl.multiple_of(yi * CH + 128 * j, 128), 128)] = w.astype(BF16)
 
     def weights(yi):
-        lax.fori_loop(0, NX * NC, lambda b, _: (second(yi, b), 0)[1], 0)
+        for b in range(NX * NC):
+            second(yi, b)
 
     def user_dot(d):
         w = W[:, :, :, span(yy[d])].reshape(NC * NX * ITM, CH)
@@ -310,54 +332,59 @@
         h = 1 - i
         k = 2 * i + h
         code(UG[d, H * h : H * h + H], QY1.at[k], MY1.at[k])
-        send2(QY1.at[k], YQ1.at[k], MY1.at[k], YM1.at[k], s_y1, k, dev(dy=d))
+        send2(QY1.at[k], YQ1.at[k], MY1.at[k], YM1.at[k], s_y1, 0, dev(dy=d))
 
     def relayed(d, i):
         h = i
         k = 2 * i + h
         arrived2(YQ2.at[i], YM2.at[i], s_y2, i)
         code(UG[d, H * h : H * h + H] + decode(YQ2[i], YM2[i]), QY1.at[k], MY1.at[k])
-        send2(QY1.at[k], YQ1.at[k], MY1.at[k], YM1.at[k], s_y1, k, dev(dy=d))
+        send2(QY1.at[k], YQ1.at[k], MY1.at[k], YM1.at[k], s_y1, 0, dev(dy=d))
 
     user_terms(1)
     direct(1, 0)
     user_terms(3)
     direct(3, 1)
-    weights(yy[0])
-    relayed(1, 0)
-    relayed(3, 1)
-
     everyone = NY * NZ * ROW
 
     def item_terms(bc, bx):
         w = W[bc, bx]
         G[bc * NX + bx] = jnp.dot(w, U[...].reshape(everyone, E), preferred_element_type=F32)
 
-    for dx in (2, 1, 3, 0):
+    def partner_terms(dx):
         item_terms(co, xx[dx])
         b = co * NX + xx[dx]
         code(G[b], QP.at[dx], MP.at[dx])
         send2(QP.at[dx], PQ.at[dx], MP.at[dx], PM.at[dx], s_pg, dx, dev(dc=1))
-    user_dot(0)
-
-    def own_terms(dx):
+
+    def add_partner(dx):
         b = c * NX + xx[dx]
-        item_terms(c, xx[dx])
         arrived2(PQ.at[dx], PM.at[dx], s_pg, dx)
         G[b] += decode(PQ[dx], PM[dx])
         return b
 
-    b2 = own_terms(2)
+    def own_terms(dx):
+        item_terms(c, xx[dx])
+        return add_partner(dx)
+
+    weights(yy[0])
+    partner_terms(2)
+    relayed(1, 0)
+    relayed(3, 1)
+    item_terms(c, xx[2])
+    partner_terms(1)
+    b2 = add_partner(2)
     for i in range(2):
         code(G[b2, H * i : H * i + H], QX2.at[i], MX2.at[i])
         send2(QX2.at[i], XQ2.at[i], MX2.at[i], XM2.at[i], s_x2, i, dev(dx=1 + 2 * i))
+    partner_terms(3)
 
     def x_direct(dx, i):
         b = own_terms(dx)
         h = 1 - i
         k = 2 * i + h
         code(G[b, H * h : H * h + H], QX1.at[k], MX1.at[k])
-        send2(QX1.at[k], XQ1.at[k], MX1.at[k], XM1.at[k], s_x1, k, dev(dx=dx))
+        send2(QX1.at[k], XQ1.at[k], MX1.at[k], XM1.at[k], s_x1, 0, dev(dx=dx))
         return b
 
     def x_relayed(b, dx, i):
@@ -365,29 +392,30 @@
         k = 2 * i + h
         arrived2(XQ2.at[i], XM2.at[i], s_x2, i)
         code(G[b, H * h : H * h + H] + decode(XQ2[i], XM2[i]), QX1.at[k], MX1.at[k])
-        send2(QX1.at[k], XQ1.at[k], MX1.at[k], XM1.at[k], s_x1, k, dev(dx=dx))
-
+        send2(QX1.at[k], XQ1.at[k], MX1.at[k], XM1.at[k], s_x1, 0, dev(dx=dx))
+
+    user_dot(0)
     b1 = x_direct(1, 0)
-    b3 = x_direct(3, 1)
     total = []
+    arrived2(YQ1, YM1, s_y1, 0)
     for h in range(2):
         v = UG[0, H * h : H * h + H]
         for i in range(2):
             k = 2 * i + h
-            arrived2(YQ1.at[k], YM1.at[k], s_y1, k)
             v = v + decode(YQ1[k], YM1[k])
         UG[0, H * h : H * h + H] = v
     UZ[...] = UG[0].T.reshape(NZ, ROW, E)
     for d in (4, 3, 5, 2, 6, 1, 7):
         code(UZ[zz[d], 0:OWN], QZ.at[d], MZ.at[d])
-        send2(QZ.at[d], ZQ.at[d], MZ.at[d], ZM.at[d], s_zr, d, dev(dz=d))
-
+        send2(QZ.at[d], ZQ.at[d], MZ.at[d], ZM.at[d], s_zr, 0, dev(dz=d))
+
+    partner_terms(0)
+    b3 = x_direct(3, 1)
     x_relayed(b1, 1, 0)
     x_relayed(b3, 3, 1)
     b0 = own_terms(0)
 
-    for d in (1, 7, 2, 6, 3, 5, 4):
-        arrived(ZPT.at[zz[d]], s_zp.at[zz[d]])
+    arrived(ZPT.at[pl.ds(0, NZ - 1)], s_zp.at[0])
     pos = ZPT[0]
     for k in range(1, NZ):
         pos = pos + ZPT[k]
@@ -402,17 +430,17 @@
     loss_out[...] = OL[...]
 
     total = UZ[z, 0:OWN]
-    for d in (1, 7, 2, 6, 3, 5, 4):
-        arrived2(ZQ.at[d], ZM.at[d], s_zr, d)
+    arrived2(ZQ.at[pl.ds(1, NZ - 1)], ZM.at[pl.ds(1, NZ - 1)], s_zr, 0)
+    for d in range(1, NZ):
         total = total + decode(ZQ[d], ZM[d])
     OU[...] = total
     ug_out[...] = OU[...]
 
+    arrived2(XQ1, XM1, s_x1, 0)
     for h in range(2):
         v = G[b0, H * h : H * h + H]
         for i in range(2):
             k = 2 * i + h
-            arrived2(XQ1.at[k], XM1.at[k], s_x1, k)
             v = v + decode(XQ1[k], XM1[k])
         OI[H * h : H * h + H] = v
         ig_out[H * h : H * h + H] = OI[H * h : H * h + H]
@@ -445,8 +473,8 @@
         V((E, NX * NC * ITM), BF16),
         V((NY, E, CH), BF16),
         V((NY, 2, 1, CH), F32),
-        V((ITM, CH), F32),
-        V((ITM, CH), F32),
+        V((2 * ITM, CH), F32),
+        V((2 * ITM, CH), F32),
         V((NX * NC, NY, ITM, CH), F32),
         V((NY, NX * NC, 1, CH), F32),
         V((NY, NX * NC, 1, CH), F32),
@@ -480,8 +508,8 @@
         D((1,)),
         D((NY * NZ,)),
         D((2 * NX * NC,)),
-        D((NY,)), D((NY,)), D((NZ,)), D((NZ,)),
-        D((2, 2)), D((4, 2)), D((NZ, 2)), D((NX, 2)), D((2, 2)), D((4, 2)),
+        D((1,)), D((1,)), D((1,)), D((1,)),
+        D((2, 2)), D((1, 2)), D((1, 2)), D((NX, 2)), D((2, 2)), D((1, 2)),
     ]
     outs = (
         jax.ShapeDtypeStruct((1, 128), F32),

time: 57.7 us -> 52.7 us (0.913)
  Pallas kernels: 57 us -> 51.8 us
    pallas_call x1, Pallas kernels: 55.7 us -> 50.5 us  [local(): pl.pallas_call(kernel, out_shape=tuple((pltpu.VMEM(o.shape, o.dtype) for...]
where the time goes in v4:
time: 52.7 us; the launch traced here: 52.6 us
  Pallas kernels  51.8 us (98%)
  between operations  0.8 us (2%)
    pallas_call x1, Pallas kernels, local(): pl.pallas_call(kernel, out_shape=tuple((pltpu.VMEM(o.shape, o.dtype) for...  50.5 us
    pallas_call x1, Pallas kernels, local(): pl.pallas_call(finish, out_shape=(jax.ShapeDtypeStruct((OWN,), F32), *out...  1.24 us

profile of v4, /device:TPU:2, one launch (start us, length us, event | category | flops | bytes accessed | tf_op | source)
XLA Modules:
  0.0 52.6 jit_solution(16720980230476961051)
XLA Ops:
  0.6 50.5 %infonce.1 = (f32[1,128]{1,0:T(1,128)S(1)}, f32[40,256]{1,0:T(8,128)S(1)}, f32[256,256]{1,0:T(8,128)S(1)}) custom-call(bf16[40,256]{1,0:T(8,128)(2,1)} %users.1, bf16[256,256]{1,0:T(8,128)(2,1)} %items.1, s32[1,40]{1,0:T(1,128)} %bitcast.1), custom_call_target="tpu_custom_call" | custom-call | tf_op jit(solution)/shard_map/infonce/pallas_call | solution.py:520
  51.2 1.2 %finish.1 = (f32[40]{0:T(128)}, f32[40,256]{1,0:T(8,128)}, f32[256,256]{1,0:T(8,128)}) custom-call(f32[1,128]{1,0:T(1,128)S(1)} %get-tuple-element.6.loss, f32[40,256]{1,0:T(8,128)S(1)} %get-tuple-element.7.ug, f32[256,256]{1,0:T(8,128)S(1)} %get-tuple-element.8.ig), custom_call_target="tpu_custom_call" | custom-call | tf_op jit(solution)/shard_map/finish/pallas_call | solution.py:531

commit v5 on v4

--- a/solution.py
+++ b/solution.py
@@ -34,9 +34,9 @@
     return q.astype(F32) * (m * (1.0 / TOP))
 
 
-def kernel(users, items, ids, loss_out, ug_out, ig_out, U, I, ID, IT, UT, HL, LGA, LGB, EX, MB, SB, PB, W, ST, PT, YST, YPT, ZST, ZPT,
-           SC, UG, UZ, QY2, MY2, QY1, MY1, YQ2, YM2, YQ1, YM1, QZ, MZ, ZQ, ZM, G, QP, MP, PQ, PM, QX2, MX2, QX1, MX1, XQ2, XM2,
-           XQ1, XM1, OL, OU, OI, s_in, s_out, s_send, s_u, s_i, s_ys, s_yp, s_zs, s_zp, s_y2, s_y1, s_zr, s_pg, s_x2, s_x1):
+def kernel(users, items, ids, loss_out, ug_out, ig_out, U, I, ID, IDS, IT, UT, HL, LGA, LGB, EX, MB, SB, PB, W, ST, PT, YST, YPT, ZST, ZPT,
+           SC, UG, QY2, MY2, QY1, MY1, YQ2, YM2, YQ1, YM1, QZ, MZ, ZQ, ZM, G, QP, MP, PQ, PM, QX2, MX2, QX1, MX1, XQ2, XM2,
+           XQ1, XM1, OL, OU, OI, s_in, s_out, s_send, s_iz, s_iy, s_u, s_i, s_ys, s_yp, s_zs, s_zp, s_y2, s_y1, s_zr, s_pg, s_x2, s_x1):
     xh, z, xl, y, c = (lax.axis_index(a) for a in AXES)
     x = 2 * xh + xl
 
@@ -82,6 +82,7 @@
     ]
     for copy in inputs:
         copy.start()
+    U[:, OWN:ROW] = jnp.zeros((NY * NZ, ROW - OWN, E), BF16)
     barrier = pltpu.get_barrier_semaphore()
     peers = [dict(dz=d) for d in range(1, NZ)] + [dict(dy=d) for d in range(1, NY)]
     peers += [dict(dx=1), dict(dx=3), dict(dc=1)]
@@ -90,13 +91,8 @@
 
     for copy in inputs:
         copy.wait()
-    PB[0, 0] = jnp.zeros((1, CH), F32)
-    PB[1, 0] = jnp.zeros((1, CH), F32)
-    PB[0, 0, :, 0:OWN] = (ID[...] >> 8).astype(F32)
-    PB[1, 0, :, 0:OWN] = (ID[...] & 255).astype(F32)
-    r8 = lax.broadcasted_iota(jnp.int32, (ROW - OWN, E), 0)
-    pad = jnp.where(r8 == 0, PB[0, 0, :, 0:E], jnp.where(r8 == 1, PB[1, 0, :, 0:E], 0.0))
-    U[mine, OWN:ROW] = pad.astype(BF16)
+    IDS[mine] = jnp.zeros((1, 128), jnp.int32)
+    IDS[mine, :, 0:OWN] = ID[...]
     pl.semaphore_wait(barrier, len(peers))
 
     H = ITM // 2
@@ -104,10 +100,19 @@
     def halves(b, order=(0, 1)):
         return [(h, I.at[b, pl.ds(h * H, H)], s_i.at[2 * b + h]) for h in order]
 
+    def send_users(s, where):
+        block = U.at[s, pl.ds(0, OWN)]
+        send(block, block, s_u.at[s], where)
+
+    def users_arrived(s):
+        arrived(U.at[s, pl.ds(0, OWN)], s_u.at[s])
+
     for d in (1, 7, 2, 6, 3, 5, 4):
-        send(U.at[mine], U.at[mine], s_u.at[mine], dev(dz=d))
+        send_users(mine, dev(dz=d))
     for d in (1, 3):
-        send(U.at[mine], U.at[mine], s_u.at[mine], dev(dy=d))
+        send_users(mine, dev(dy=d))
+    for d in range(1, NZ):
+        send(IDS.at[mine], IDS.at[mine], s_iz.at[0], dev(dz=d))
     for dx, order in ((1, (0, 1)), (3, (1, 0))):
         for h, dst, sem in halves(bo, order):
             send(dst, dst, sem, dev(dx=dx))
@@ -116,7 +121,8 @@
 
     def place_ids(yi):
         UT[yi] = U[pl.ds(yi * NZ, NZ)].reshape(CH, E).T
-        part = U[pl.ds(yi * NZ, NZ), OWN:ROW, 0:128].astype(F32)
+        part = IDS[pl.ds(yi * NZ, NZ)].reshape(NZ, 128)
+        parts = (part >> 8, part & 255)
         n = lax.broadcasted_iota(jnp.int32, (128, CH), 1)
         k = (n * 1366) >> 16
         pick = jnp.where(n - k * ROW == lax.broadcasted_iota(jnp.int32, (128, CH), 0), 1.0, 0.0)
@@ -125,7 +131,7 @@
         k8 = (n8 * 1366) >> 16
         here = k8 == lax.broadcasted_iota(jnp.int32, (NZ, CH), 0)
         for j in range(2):
-            spread = jnp.dot(part[:, j, :].astype(BF16), pick, preferred_element_type=F32)
+            spread = jnp.dot(parts[j].astype(F32).astype(BF16), pick, preferred_element_type=F32)
             HL[yi, j] = jnp.sum(jnp.where(here, spread, 0.0), axis=0, keepdims=True)
 
     n1 = lax.broadcasted_iota(jnp.int32, (1, CH), 1)
@@ -185,16 +191,16 @@
 
     def from_z(d):
         s = y * NZ + zz[d]
-        arrived(U.at[s], s_u.at[s])
+        users_arrived(s)
         for dy in (1, 3):
-            send(U.at[s], U.at[s], s_u.at[s], dev(dy=dy))
+            send_users(s, dev(dy=dy))
 
     def from_y(d):
         for dy in (3, 1):
             s = yy[dy] * NZ + zz[d]
-            arrived(U.at[s], s_u.at[s])
+            users_arrived(s)
             if (d in UP) == (dy == 3):
-                send(U.at[s], U.at[s], s_u.at[s], dev(dy=4 - dy))
+                send_users(s, dev(dy=4 - dy))
 
     def from_x(step):
         for dx, keep in ((3, 0), (1, 1)):
@@ -216,31 +222,35 @@
             arrived(ref, sem)
         return b
 
-    for d in (1, 7, 2, 6):
+    for d in (1, 7, 2):
         from_z(d)
+    from_x(0)
+    from_z(6)
     from_y(0)
-    from_x(0)
-    for d in (3, 5, 4):
-        from_z(d)
+    from_z(3)
     from_x(1)
+    from_z(5)
+    from_z(4)
+    arrived(IDS.at[pl.ds(0, NZ - 1)], s_iz.at[0])
+    these = IDS.at[pl.ds(y * NZ, NZ)]
+    for dy in (1, 3, 2):
+        send(these, these, s_iy.at[0], dev(dy=dy))
     place_ids(yy[0])
     first_some(yy[0], [c * NX + xx[dx] for dx in (0, 3, 1)])
-    from_y(1)
-    from_y(7)
+    first_some(yy[0], [from_partner(dx) for dx in (0, 3, 1)])
+    for d in (1, 7):
+        from_y(d)
     from_x2()
-    from_y(2)
-    from_y(6)
-    first_some(yy[0], [from_partner(dx) for dx in (0, 3, 1)])
-    for d in (3, 5, 4):
+    for d in (2, 6, 3, 5, 4):
         from_y(d)
     first_some(yy[0], [c * NX + xx[2], from_partner(2)])
 
+    arrived(IDS.at[pl.ds(0, (NY - 1) * NZ)], s_iy.at[0])
     for dy in (3, 1):
         place_ids(yy[dy])
         first_all(yy[dy])
     for d in range(NZ):
-        s = yy[2] * NZ + d
-        arrived(U.at[s], s_u.at[s])
+        users_arrived(yy[2] * NZ + d)
     place_ids(yy[2])
     first_all(yy[2])
 
@@ -306,14 +316,17 @@
 
     def user_dot(d):
         w = W[:, :, :, span(yy[d])].reshape(NC * NX * ITM, CH)
-        UG[d] = jnp.dot(IT[...], w, preferred_element_type=F32)
+        UG[d] = jnp.dot(IT[...], w, preferred_element_type=F32).T.reshape(NZ, ROW, E)
 
     def user_terms(d):
         weights(yy[d])
         user_dot(d)
 
-    H = E // 2
-    half = [pl.ds(0, H), pl.ds(H, H)]
+    H = ITM // 2
+    HZ = NZ // 2
+
+    def part(d, h):
+        return UG[d, HZ * h : HZ * h + HZ, 0:OWN].reshape(HZ * OWN, E)
 
     def send2(q, qto, m, mto, recv, i, where):
         send(q, qto, recv.at[i, 0], where)
@@ -325,20 +338,20 @@
 
     user_terms(2)
     for i in range(2):
-        code(UG[2, H * i : H * i + H], QY2.at[i], MY2.at[i])
+        code(part(2, i), QY2.at[i], MY2.at[i])
         send2(QY2.at[i], YQ2.at[i], MY2.at[i], YM2.at[i], s_y2, i, dev(dy=1 + 2 * i))
 
     def direct(d, i):
         h = 1 - i
         k = 2 * i + h
-        code(UG[d, H * h : H * h + H], QY1.at[k], MY1.at[k])
+        code(part(d, h), QY1.at[k], MY1.at[k])
         send2(QY1.at[k], YQ1.at[k], MY1.at[k], YM1.at[k], s_y1, 0, dev(dy=d))
 
     def relayed(d, i):
         h = i
         k = 2 * i + h
         arrived2(YQ2.at[i], YM2.at[i], s_y2, i)
-        code(UG[d, H * h : H * h + H] + decode(YQ2[i], YM2[i]), QY1.at[k], MY1.at[k])
+        code(part(d, h) + decode(YQ2[i], YM2[i]), QY1.at[k], MY1.at[k])
         send2(QY1.at[k], YQ1.at[k], MY1.at[k], YM1.at[k], s_y1, 0, dev(dy=d))
 
     user_terms(1)
@@ -396,17 +409,15 @@
 
     user_dot(0)
     b1 = x_direct(1, 0)
-    total = []
     arrived2(YQ1, YM1, s_y1, 0)
     for h in range(2):
-        v = UG[0, H * h : H * h + H]
+        v = part(0, h)
         for i in range(2):
             k = 2 * i + h
             v = v + decode(YQ1[k], YM1[k])
-        UG[0, H * h : H * h + H] = v
-    UZ[...] = UG[0].T.reshape(NZ, ROW, E)
+        UG[0, HZ * h : HZ * h + HZ, 0:OWN] = v.reshape(HZ, OWN, E)
     for d in (4, 3, 5, 2, 6, 1, 7):
-        code(UZ[zz[d], 0:OWN], QZ.at[d], MZ.at[d])
+        code(UG[0, zz[d], 0:OWN], QZ.at[d], MZ.at[d])
         send2(QZ.at[d], ZQ.at[d], MZ.at[d], ZM.at[d], s_zr, 0, dev(dz=d))
 
     partner_terms(0)
@@ -429,7 +440,7 @@
     OL[:, ROW:128] = jnp.zeros((1, 128 - ROW), F32)
     loss_out[...] = OL[...]
 
-    total = UZ[z, 0:OWN]
+    total = UG[0, z, 0:OWN]
     arrived2(ZQ.at[pl.ds(1, NZ - 1)], ZM.at[pl.ds(1, NZ - 1)], s_zr, 0)
     for d in range(1, NZ):
         total = total + decode(ZQ[d], ZM[d])
@@ -466,10 +477,12 @@
     D = pltpu.SemaphoreType.DMA
     I16 = jnp.int16
     HE = E // 2
+    HU = NZ // 2 * OWN
     scratch = [
         V((NY * NZ, ROW, E), BF16),
         V((NX * NC, ITM, E), BF16),
         V((1, OWN), jnp.int32),
+        V((NY * NZ, 1, 128), jnp.int32),
         V((E, NX * NC * ITM), BF16),
         V((NY, E, CH), BF16),
         V((NY, 2, 1, CH), F32),
@@ -487,12 +500,11 @@
         V((NZ, 16, 128), F32),
         V((NZ, 8, 128), F32),
         V((NY, 1, CH), F32),
-        V((NY, E, CH), F32),
-        V((NZ, ROW, E), F32),
-        V((2, HE, CH), I16), V((2, 1, CH), F32),
-        V((4, HE, CH), I16), V((4, 1, CH), F32),
-        V((2, HE, CH), I16), V((2, 1, CH), F32),
-        V((4, HE, CH), I16), V((4, 1, CH), F32),
+        V((NY, NZ, ROW, E), F32),
+        V((2, HU, E), I16), V((2, 1, E), F32),
+        V((4, HU, E), I16), V((4, 1, E), F32),
+        V((2, HU, E), I16), V((2, 1, E), F32),
+        V((4, HU, E), I16), V((4, 1, E), F32),
         V((NZ, OWN, E), I16), V((NZ, 1, E), F32),
         V((NZ, OWN, E), I16), V((NZ, 1, E), F32),
         V((NX * NC, ITM, E), F32),
@@ -505,6 +517,8 @@
         V((1, 128), F32), V((OWN, E), F32), V((ITM, E), F32),
         D((3,)),
         D((4,)),
+        D((1,)),
+        D((1,)),
         D((1,)),
         D((NY * NZ,)),
         D((2 * NX * NC,)),

time: 52.7 us -> 52.2 us (level)
  no operation moved by 1% of the time
where the time goes in v5:
time: 52.2 us; the launch traced here: 52.1 us
  Pallas kernels  51.3 us (98%)
  between operations  0.8 us (2%)
    pallas_call x1, Pallas kernels, local(): pl.pallas_call(kernel, out_shape=tuple((pltpu.VMEM(o.shape, o.dtype) for...  50 us
    pallas_call x1, Pallas kernels, local(): pl.pallas_call(finish, out_shape=(jax.ShapeDtypeStruct((OWN,), F32), *out...  1.24 us

profile of v5, /device:TPU:2, one launch (start us, length us, event | category | flops | bytes accessed | tf_op | source)
XLA Modules:
  0.0 52.1 jit_solution(4268065476957870225)
XLA Ops:
  0.6 50.0 %infonce.1 = (f32[1,128]{1,0:T(1,128)S(1)}, f32[40,256]{1,0:T(8,128)S(1)}, f32[256,256]{1,0:T(8,128)S(1)}) custom-call(bf16[40,256]{1,0:T(8,128)(2,1)} %users.1, bf16[256,256]{1,0:T(8,128)(2,1)} %items.1, s32[1,40]{1,0:T(1,128)} %bitcast.1), custom_call_target="tpu_custom_call" | custom-call | tf_op jit(solution)/shard_map/infonce/pallas_call | solution.py:534
  50.7 1.2 %finish.1 = (f32[40]{0:T(128)}, f32[40,256]{1,0:T(8,128)}, f32[256,256]{1,0:T(8,128)}) custom-call(f32[1,128]{1,0:T(1,128)S(1)} %get-tuple-element.6.loss, f32[40,256]{1,0:T(8,128)S(1)} %get-tuple-element.7.ug, f32[256,256]{1,0:T(8,128)S(1)} %get-tuple-element.8.ig), custom_call_target="tpu_custom_call" | custom-call | tf_op jit(solution)/shard_map/finish/pallas_call | solution.py:545
